TPU v7x, 8 devices: a whole 2x2x1 slice. The times are simulated.
8 devices in a mesh: tp: 2 (over z, y), ep: 4 (over x, core).
Axes of the slice: x: 2, y: 2, z: 1, core: 2. Of those that a mesh axis runs over, the one named last changes fastest.
Arguments:
- x_tok: bfloat16 [32768, 512], P('ep')
- dy_tok: bfloat16 [32768, 512], P('ep')
- route_idx: int32 [32768, 2], P('ep')
- norm_scale: float32 [512], replicated
- w_router: float32 [512, 32], replicated
- w_gate: bfloat16 [32, 512, 2048], P('ep', None, 'tp')
- w_lin: bfloat16 [32, 512, 2048], P('ep', None, 'tp')
- w_out: bfloat16 [32, 2048, 512], P('ep', 'tp')
Outputs:
- output 1: bfloat16 [32768, 512], P('ep')
- output 2: float32 [2], replicated
- output 3: bfloat16 [32768, 512], P('ep')
- output 4: float32 [512], replicated
- output 5: float32 [512, 32], replicated
- output 6: float32 [32, 512, 2048], P('ep', None, 'tp')
- output 7: float32 [32, 512, 2048], P('ep', None, 'tp')
- output 8: float32 [32, 2048, 512], P('ep', 'tp')
All inputs are finite; a program needn't handle non-finite values.
Results may differ from a plain program's by a relative error of at most 0.0154704.
Values are sent between devices in bfloat16 or wider.
A program may use at most 1 GiB of HBM per device.

v0:
```python
import jax
import jax.numpy as jnp
from jax import lax
from jax.sharding import PartitionSpec as P

NORM_EPS = 1e-6
Z_COEF = 0.001
AUX_COEF = 0.01


def gelu_fn(pre_act):
    return jax.nn.gelu(pre_act, approximate=True)


def route_slots(route_ids, experts, slot_cap, stride):
    expert_ids = jnp.arange(experts, dtype=jnp.int32)
    hit_first = (route_ids[:, 0:1] == expert_ids).astype(jnp.int32)
    hit_second = (route_ids[:, 1:2] == expert_ids).astype(jnp.int32)
    rank_first = jnp.cumsum(hit_first, axis=0) - hit_first
    rank_second = jnp.cumsum(hit_second, axis=0) - hit_second + jnp.sum(hit_first, axis=0)
    pos_first = jnp.sum(rank_first * hit_first, axis=1)
    pos_second = jnp.sum(rank_second * hit_second, axis=1)
    overflow = experts * stride
    slot_first = jnp.where(pos_first < slot_cap, route_ids[:, 0] * stride + pos_first, overflow)
    slot_second = jnp.where(pos_second < slot_cap, route_ids[:, 1] * stride + pos_second, overflow)
    return slot_first, slot_second


def slot_tables(slot_first, slot_second, gate_first, gate_second, slot_total):
    tok_count = slot_first.shape[0]
    tok_ids = jnp.arange(tok_count, dtype=jnp.int32)
    slot_tok = jnp.full((slot_total + 1,), tok_count, jnp.int32)
    slot_tok = slot_tok.at[slot_first].set(tok_ids).at[slot_second].set(tok_ids)
    slot_gate = jnp.zeros((slot_total + 1,), jnp.float32)
    slot_gate = slot_gate.at[slot_first].set(gate_first).at[slot_second].set(gate_second)
    return slot_tok[:slot_total], slot_gate[:slot_total]


def pick_rows(row_data, slot_index):
    return jnp.take(row_data, slot_index, axis=0, mode='fill', fill_value=0)


def solution(mesh):
    ep_size = mesh.shape['ep']

    def device_block(x_loc, dy_loc, idx_loc, norm_scale, w_router, gate_loc, lin_loc, out_loc):
        tok_count, model_width = x_loc.shape
        experts = w_router.shape[1]
        local_exp = gate_loc.shape[0]
        tokens = tok_count * ep_size
        slot_cap = (5 * tok_count + 2 * experts - 1) // (2 * experts)
        x_wide = x_loc.astype(jnp.float32)
        inv_rms = lax.rsqrt(jnp.mean(x_wide * x_wide, axis=-1, keepdims=True) + NORM_EPS)
        x_norm = x_wide * inv_rms
        u_tok = (x_norm * norm_scale).astype(jnp.bfloat16)
        u_wide = u_tok.astype(jnp.float32)
        logits = jnp.dot(u_wide, w_router, preferred_element_type=jnp.float32)
        log_norm = jax.nn.logsumexp(logits, axis=-1)
        router_prob = jnp.exp(logits - log_norm[:, None])
        expert_ids = jnp.arange(experts, dtype=jnp.int32)
        one_first = (idx_loc[:, 0:1] == expert_ids).astype(jnp.float32)
        one_second = (idx_loc[:, 1:2] == expert_ids).astype(jnp.float32)
        first_count = lax.psum(jnp.sum(one_first, axis=0), 'ep')
        prob_sum = lax.psum(jnp.sum(router_prob, axis=0), 'ep')
        norm_sq = lax.psum(jnp.sum(log_norm * log_norm), 'ep')
        frac_first = first_count / tokens
        z_loss = Z_COEF * norm_sq / tokens
        aux_loss = AUX_COEF * experts * jnp.sum(frac_first * prob_sum) / tokens
        gate_first = jnp.sum(router_prob * one_first, axis=-1)
        gate_second = jnp.sum(router_prob * one_second, axis=-1)
        gate_total = gate_first + gate_second
        norm_first = gate_first / gate_total
        norm_second = gate_second / gate_total
        slot_first, slot_second = route_slots(idx_loc, experts, slot_cap, slot_cap)
        slot_tok, slot_gate = slot_tables(slot_first, slot_second, norm_first, norm_second, experts * slot_cap)
        disp_rows = pick_rows(u_tok, slot_tok).reshape(experts, slot_cap, model_width)
        recv_rows = lax.all_to_all(disp_rows, 'ep', 0, 0, tiled=True).reshape(ep_size, local_exp, slot_cap, model_width)
        a_gate = jnp.einsum('sxcd,xdf->sxcf', recv_rows, gate_loc, preferred_element_type=jnp.float32)
        a_lin = jnp.einsum('sxcd,xdf->sxcf', recv_rows, lin_loc, preferred_element_type=jnp.float32)
        gelu_val, gelu_back = jax.vjp(gelu_fn, a_gate)
        hidden = (gelu_val * a_lin).astype(jnp.bfloat16)
        part_out = jnp.einsum('sxcf,xfd->sxcd', hidden, out_loc, preferred_element_type=jnp.float32).astype(jnp.bfloat16)
        exp_out = lax.psum(part_out, 'tp')
        back_rows = lax.all_to_all(exp_out.reshape(experts, slot_cap, model_width), 'ep', 0, 0, tiled=True).reshape(experts * slot_cap, model_width)
        out_first = pick_rows(back_rows, slot_first).astype(jnp.float32)
        out_second = pick_rows(back_rows, slot_second).astype(jnp.float32)
        y_loc = (x_wide + norm_first[:, None] * out_first + norm_second[:, None] * out_second).astype(jnp.bfloat16)
        dy_wide = dy_loc.astype(jnp.float32)
        dn_first = jnp.sum(dy_wide * out_first, axis=-1)
        dn_second = jnp.sum(dy_wide * out_second, axis=-1)
        do_slot = (pick_rows(dy_loc, slot_tok).astype(jnp.float32) * slot_gate[:, None]).astype(jnp.bfloat16)
        do_recv = lax.all_to_all(do_slot.reshape(experts, slot_cap, model_width), 'ep', 0, 0, tiled=True).reshape(ep_size, local_exp, slot_cap, model_width)
        d_hidden = jnp.einsum('sxcd,xfd->sxcf', do_recv, out_loc, preferred_element_type=jnp.float32)
        da_gate = gelu_back(d_hidden * a_lin)[0].astype(jnp.bfloat16)
        da_lin = (d_hidden * gelu_val).astype(jnp.bfloat16)
        d_out = jnp.einsum('sxcf,sxcd->xfd', hidden, do_recv, preferred_element_type=jnp.float32)
        d_gate = jnp.einsum('sxcd,sxcf->xdf', recv_rows, da_gate, preferred_element_type=jnp.float32)
        d_lin = jnp.einsum('sxcd,sxcf->xdf', recv_rows, da_lin, preferred_element_type=jnp.float32)
        du_part = jnp.einsum('sxcf,xdf->sxcd', da_gate, gate_loc, preferred_element_type=jnp.float32) + jnp.einsum('sxcf,xdf->sxcd', da_lin, lin_loc, preferred_element_type=jnp.float32)
        du_slot = lax.psum(du_part.astype(jnp.bfloat16), 'tp')
        du_back = lax.all_to_all(du_slot.reshape(experts, slot_cap, model_width), 'ep', 0, 0, tiled=True).reshape(experts * slot_cap, model_width)
        du_exp = pick_rows(du_back, slot_first).astype(jnp.float32) + pick_rows(du_back, slot_second).astype(jnp.float32)
        gate_mix = norm_first * dn_first + norm_second * dn_second
        aux_coef = AUX_COEF * experts * frac_first
        d_logits = router_prob * (aux_coef - jnp.sum(aux_coef * router_prob, axis=-1, keepdims=True))
        d_logits = d_logits + (2.0 * Z_COEF) * log_norm[:, None] * router_prob
        d_logits = d_logits + one_first * (norm_first * (dn_first - gate_mix))[:, None]
        d_logits = d_logits + one_second * (norm_second * (dn_second - gate_mix))[:, None]
        d_router = lax.psum(jnp.einsum('td,te->de', u_wide, d_logits, preferred_element_type=jnp.float32), 'ep')
        du_all = du_exp + jnp.einsum('te,de->td', d_logits, w_router, preferred_element_type=jnp.float32)
        d_scale = lax.psum(jnp.sum(du_all * x_norm, axis=0), 'ep')
        dx_norm = du_all * norm_scale
        dx_loc = (dy_wide + inv_rms * (dx_norm - x_norm * jnp.mean(dx_norm * x_norm, axis=-1, keepdims=True))).astype(jnp.bfloat16)
        losses = jnp.stack([z_loss, aux_loss])
        return (y_loc, losses, dx_loc, d_scale, d_router, d_gate, d_lin, d_out)

    tok_spec = P('ep', None)
    in_spec = P('ep', None, 'tp')
    out_spec = P('ep', 'tp', None)
    return jax.shard_map(device_block, mesh=mesh, in_specs=(tok_spec, tok_spec, tok_spec, P(), P(), in_spec, in_spec, out_spec), out_specs=(tok_spec, P(), tok_spec, P(), P(), in_spec, in_spec, out_spec), check_vma=False)
```

profile of v0, /device:TPU:0, one launch (start us, length us, event | category | flops | bytes accessed | tf_op | source)
XLA Modules:
  0.0 2676.9 jit_solution(11063232838826841255)
XLA Ops:
  8.3 9.5 reduce-window.14
  33.4 30.5 %scatter_custom_fusion = s32[20481]{0:T(1024)S(1)} fusion(s32[8192]{0:T(1024)S(1)} %bitcast.156, s32[8192]{0:T(1024)S(1)} %iota.18, s32[]{:T(128)} %constant.39.clone.1), kind=kCustom, calls=%fused_computation.124 | custom fusion | bytes 81928 | tf_op jit(solution)/shard_map/scatter | solution.py:33
  63.9 30.5 %scatter_fusion = s32[20481]{0:T(1024)S(1)} fusion(s32[20481]{0:T(1024)S(1)} %scatter_custom_fusion, s32[8192]{0:T(1024)S(1)} %bitcast.152, s32[8192]{0:T(1024)S(1)} %iota.19), kind=kCustom, calls=%fused_computation.7 | custom fusion | bytes 131072 | tf_op jit(solution)/shard_map/scatter | solution.py:33
  107.5 87.4 %gather_fusion = bf16[20480,512]{1,0:T(8,128)(2,1)} fusion(bf16[8192,512]{1,0:T(8,128)(2,1)} %fusion.30, s32[20480]{0:T(1024)S(1)} %fusion.65), kind=kCustom, calls=%fused_computation.clone | custom fusion | bytes 42024960 | tf_op jit(solution)/shard_map/jit(_take)/gather | solution.py:40
  194.9 17.9 broadcast_select_fusion
  221.0 229.1 %psum.51 = f32[32]{0:T(128)S(1)} all-reduce(f32[32]{0:T(128)S(1)} %convert_reduce_fusion.1), channel_id=1, replica_groups=mesh['tp'=2,'ep'=4] {'ep'}, use_global_device_ids=true, to_apply=%region_18.21 | all-reduce | flops 32 | bytes 256 | tf_op jit(solution)/shard_map/psum | solution.py:63
  458.3 30.5 %scatter_custom_fusion.2 = f32[20481]{0:T(1024)S(1)} fusion(s32[8192]{0:T(1024)S(1)} %bitcast.157, f32[8192]{0:T(1024)S(1)} %get-tuple-element.35, f32[]{:T(128)} %constant.23.clone.1), kind=kCustom, calls=%fused_computation.122 | custom fusion | bytes 81928 | tf_op jit(solution)/shard_map/scatter | solution.py:35
  488.8 30.5 %scatter_fusion.1 = f32[20481]{0:T(1024)S(1)} fusion(f32[20481]{0:T(1024)S(1)} %scatter_custom_fusion.2, s32[8192]{0:T(1024)S(1)} %bitcast.153, f32[8192]{0:T(1024)S(1)} %get-tuple-element.36), kind=kCustom, calls=%fused_computation.9 | custom fusion | bytes 131072 | tf_op jit(solution)/shard_map/scatter | solution.py:35
  519.4 87.3 %gather_fusion.3 = bf16[20480,512]{1,0:T(8,128)(2,1)} fusion(bf16[8192,512]{1,0:T(8,128)(2,1)} %param.13, s32[20480]{0:T(1024)S(1)} %fusion.65), kind=kCustom, calls=%fused_computation.2.clone | custom fusion | bytes 42024960 | tf_op jit(solution)/shard_map/jit(_take)/gather | solution.py:40
  606.7 16.3 multiply_convert_fusion
  631.0 41.0 %fusion.24 = f32[8,4,640,1024]{3,2,1,0:T(8,128)} fusion(bf16[4,8,640,512]{3,2,1,0:T(8,128)(2,1)} %bitcast.11, bf16[8,512,1024]{2,1,0:T(8,128)(2,1)} %param.18), kind=kOutput, calls=%fused_computation.53 | convolution fusion | flops 21474836480 | bytes 113246208 | tf_op jit(solution)/shard_map/sxcd,xdf->sxcf/dot_general | solution.py:79
  672.0 41.0 %fusion.26 = f32[8,4,640,1024]{3,2,1,0:T(8,128)} fusion(bf16[4,8,640,512]{3,2,1,0:T(8,128)(2,1)} %bitcast.11, bf16[8,512,1024]{2,1,0:T(8,128)(2,1)} %param.17), kind=kOutput, calls=%fused_computation.55 | convolution fusion | flops 21474836480 | bytes 113246208 | tf_op jit(solution)/shard_map/sxcd,xdf->sxcf/dot_general | solution.py:78
  712.9 145.4 %all-to-all-done.2 = bf16[32,640,512]{2,1,0:T(8,128)(2,1)} async-done(((bf16[32,640,512]{2,1,0:T(8,128)(2,1)}), bf16[32,640,512]{2,1,0:T(8,128)(2,1)}, u32[]{:S(2)}, u32[]{:S(2)}) %all-to-all-start.2) | async-done | bytes 20971552 | tf_op jit(solution)/shard_map/all_to_all | solution.py:92
  858.4 124.5 %fusion.7 = (bf16[4,8,640,1024]{3,2,0,1:T(8,128)(2,1)}, bf16[4,8,640,1024]{3,2,0,1:T(8,128)(2,1)}, bf16[4,8,640,1024]{3,2,0,1:T(8,128)(2,1)}) fusion(f32[8,4,640,1024]{3,2,1,0:T(8,128)} %fusion.26, f32[8,4,640,1024]{3,2,1,0:T(8,128)} %fusion.24, bf16[8,1024,512]{2,1,0:T(8,128)(2,1)} %param.19, bf16[4,8,640,512]{3,2,1,0:T(8,128)(2,1)} %bitcast.26), kind=kOutput, calls=%fused_computation.21 | convolution fusion | flops 22020096000 | bytes 322961408 | tf_op jit(solution)/shard_map/sxcd,xfd->sxcf/dot_general | solution.py:93
  982.8 38.9 %fusion.50 = f32[8,4,640,512]{3,2,1,0:T(8,128)} fusion(bf16[4,8,640,1024]{3,2,0,1:T(8,128)(2,1)} %get-tuple-element.28, bf16[8,512,1024]{2,1,0:T(8,128)(2,1)} %param.17), kind=kOutput, calls=%fused_computation.74 | convolution fusion | flops 21474836480 | bytes 92274688 | tf_op jit(solution)/shard_map/sxcf,xdf->sxcd/dot_general | solution.py:99
  1021.7 41.2 %fusion.19 = bf16[4,8,640,512]{3,2,0,1:T(8,128)(2,1)} fusion(f32[8,4,640,512]{3,2,1,0:T(8,128)} %fusion.50, bf16[4,8,640,1024]{3,2,0,1:T(8,128)(2,1)} %get-tuple-element.27, bf16[8,512,1024]{2,1,0:T(8,128)(2,1)} %param.18), kind=kOutput, calls=%fused_computation.46 | convolution fusion | flops 21495808000 | bytes 113246208 | tf_op jit(solution)/shard_map/sxcf,xdf->sxcd/dot_general | solution.py:99
  1062.9 17.3 copy.23
  1080.2 31.4 %convert_bitcast_fusion = bf16[4,8,640,512]{3,2,0,1:T(8,128)(2,1)} fusion(bf16[4,8,640,1024]{3,2,0,1:T(8,128)(2,1)} %get-tuple-element.29, bf16[8,1024,512]{2,1,0:T(8,128)(2,1)} %param.19), kind=kOutput, calls=%fused_computation.47 | convolution fusion | flops 21485322240 | bytes 71303168 | tf_op jit(solution)/shard_map/sxcf,xfd->sxcd/dot_general | solution.py:82
  1111.7 17.3 copy.21
  1129.0 913.5 %all-reduce.7.cloned.1.call-done = (bf16[32,640,512]{2,1,0:T(8,128)(2,1)}, bf16[32,640,512]{2,1,0:T(8,128)(2,1)}) async-done(((bf16[32,640,512]{2,1,0:T(8,128)(2,1)}, bf16[32,640,512]{2,1,0:T(8,128)(2,1)}), (bf16[32,640,512]{2,1,0:T(8,128)(2,1)}, bf16[32,640,512]{2,1,0:T(8,128)(2,1)})) %all-reduce.7.cloned.1.call-update) | async-done | bytes 41943056 | tf_op jit(solution)/shard_map/psum | solution.py:83
  2042.6 240.5 %all_to_all.20 = bf16[32,640,512]{2,1,0:T(8,128)(2,1)} all-to-all(bf16[32,640,512]{2,1,0:T(8,128)(2,1)} %get-tuple-element.23), channel_id=1, replica_groups=mesh['tp'=2,'ep'=4] {'ep'}, dimensions={0} | all-to-all | bytes 41943040 | tf_op jit(solution)/shard_map/all_to_all | solution.py:84
  2292.3 34.0 %fusion.39 = f32[8,1024,512]{2,1,0:T(8,128)} fusion(bf16[4,8,640,1024]{3,2,0,1:T(8,128)(2,1)} %get-tuple-element.29, bf16[4,8,640,512]{3,2,1,0:T(8,128)(2,1)} %bitcast.26), kind=kOutput, calls=%fused_computation.69 | convolution fusion | flops 21474836480 | bytes 79691776 | tf_op jit(solution)/shard_map/sxcf,sxcd->xfd/dot_general | solution.py:96
  2326.3 32.5 %fusion.42 = f32[8,512,1024]{2,1,0:T(8,128)} fusion(bf16[4,8,640,512]{3,2,1,0:T(8,128)(2,1)} %bitcast.11, bf16[4,8,640,1024]{3,2,0,1:T(8,128)(2,1)} %get-tuple-element.28), kind=kOutput, calls=%fused_computation.70 | convolution fusion | flops 21474836480 | bytes 79691776 | tf_op jit(solution)/shard_map/sxcd,sxcf->xdf/dot_general | solution.py:97
  2358.8 32.7 %fusion.45 = f32[8,512,1024]{2,1,0:T(8,128)} fusion(bf16[4,8,640,512]{3,2,1,0:T(8,128)(2,1)} %bitcast.11, bf16[4,8,640,1024]{3,2,0,1:T(8,128)(2,1)} %get-tuple-element.27), kind=kOutput, calls=%fused_computation.71 | convolution fusion | flops 21474836480 | bytes 79691776 | tf_op jit(solution)/shard_map/sxcd,sxcf->xdf/dot_general | solution.py:98
  2391.5 43.4 %gather_fusion.2 = bf16[8192,512]{1,0:T(8,128)(2,1)} fusion(bf16[20480,512]{1,0:T(8,128)(2,1)} %bitcast.127, s32[8192]{0:T(1024)S(1)} %broadcast_clamp_fusion), kind=kCustom, calls=%fused_computation.3.clone | custom fusion | bytes 16809984 | tf_op jit(solution)/shard_map/jit(_take)/gather | solution.py:40
  2434.9 43.8 %gather_fusion.1 = bf16[8192,512]{1,0:T(8,128)(2,1)} fusion(bf16[20480,512]{1,0:T(8,128)(2,1)} %bitcast.128, s32[8192]{0:T(1024)S(1)} %broadcast_clamp_fusion.1), kind=kCustom, calls=%fused_computation.1.clone | custom fusion | bytes 16809984 | tf_op jit(solution)/shard_map/jit(_take)/gather | solution.py:40
  2478.8 39.9 %all-to-all-done.3 = bf16[32,640,512]{2,1,0:T(8,128)(2,1)} async-done(((bf16[32,640,512]{2,1,0:T(8,128)(2,1)}), bf16[32,640,512]{2,1,0:T(8,128)(2,1)}, u32[]{:S(2)}, u32[]{:S(2)}) %all-to-all-start.3) | async-done | bytes 20971552 | tf_op jit(solution)/shard_map/all_to_all | solution.py:101
  2518.6 43.4 %gather_fusion.5 = bf16[8192,512]{1,0:T(8,128)(2,1)} fusion(bf16[20480,512]{1,0:T(8,128)(2,1)} %bitcast.33, s32[8192]{0:T(1024)S(1)} %broadcast_clamp_fusion), kind=kCustom, calls=%fused_computation.5.clone | custom fusion | bytes 16809984 | tf_op jit(solution)/shard_map/jit(_take)/gather | solution.py:40
  2562.1 43.4 %gather_fusion.4 = bf16[8192,512]{1,0:T(8,128)(2,1)} fusion(bf16[20480,512]{1,0:T(8,128)(2,1)} %bitcast.33, s32[8192]{0:T(1024)S(1)} %broadcast_clamp_fusion.1), kind=kCustom, calls=%fused_computation.4.clone | custom fusion | bytes 16809984 | tf_op jit(solution)/shard_map/jit(_take)/gather | solution.py:40
  2605.6 15.7 fusion.36
  2627.0 17.5 fusion.34
  2651.4 14.8 fusion.38
  (115 shorter events, 77.8 us)
Async XLA Ops:
  7.2 442.9 %copy-start = (f32[512,32]{0,1:T(8,128)S(1)}, f32[512,32]{0,1:T(8,128)}, u32[]{:S(2)}) copy-start(f32[512,32]{0,1:T(8,128)} %param.16) | copy-start | bytes 196612
  8.2 448.8 %copy-start.3 = (s32[8192,1]{0,1:T(1,128)}, s32[8192,1]{0,1:T(1,128)S(1)}, u32[]{:S(2)}) copy-start(s32[8192,1]{0,1:T(1,128)S(1)} %get-tuple-element.38) | copy-start | bytes 98308
  8.2 448.8 %copy-start.6 = (s32[8192,1]{0,1:T(1,128)}, s32[8192,1]{0,1:T(1,128)S(1)}, u32[]{:S(2)}) copy-start(s32[8192,1]{0,1:T(1,128)S(1)} %get-tuple-element.37) | copy-start | bytes 98308
  32.3 62.2 %copy-start.13 = (s32[8192]{0:T(1024)}, s32[8192]{0:T(1024)S(1)}, u32[]{:S(2)}) copy-start(s32[8192]{0:T(1024)S(1)} %fusion.60) | copy-start | bytes 98308
  63.9 35.8 %copy-start.26 = (f32[512]{0:T(512)S(1)}, f32[512]{0:T(512)}, u32[]{:S(2)}) copy-start(f32[512]{0:T(512)} %param.15) | copy-start | bytes 6148
  99.6 95.2 %copy-start.20 = (f32[8192]{0:T(1024)}, f32[8192]{0:T(1024)S(1)}, u32[]{:S(2)}) copy-start(f32[8192]{0:T(1024)S(1)} %add_rsqrt_fusion) | copy-start | bytes 98308
  212.8 410.2 %all-to-all-start = ((bf16[32,640,512]{2,1,0:T(8,128)(2,1)}), bf16[32,640,512]{2,1,0:T(8,128)(2,1)}, u32[]{:S(2)}, u32[]{:S(2)}) async-start(bf16[32,640,512]{2,1,0:T(8,128)(2,1)} %bitcast.129), calls=%async_computation | async-start | bytes 41943040 | tf_op jit(solution)/shard_map/all_to_all | solution.py:77
  456.3 63.1 %copy-start.29 = (f32[32]{0:T(128)}, f32[32]{0:T(128)S(1)}, u32[]{:S(2)}) copy-start(f32[32]{0:T(128)S(1)} %broadcast_multiply_fusion.2) | copy-start | bytes 388
  457.0 62.4 %copy-start.17 = (f32[8192]{0:T(1024)}, f32[8192]{0:T(1024)S(1)}, u32[]{:S(2)}) copy-start(f32[8192]{0:T(1024)S(1)} %get-tuple-element.26) | copy-start | bytes 98308
  458.3 30.5 %copy-start.15 = (f32[8192]{0:T(1024)}, f32[8192]{0:T(1024)S(1)}, u32[]{:S(2)}) copy-start(f32[8192]{0:T(1024)S(1)} %get-tuple-element.35) | copy-start | bytes 98308
  458.3 61.1 %copy-start.9 = (f32[8192]{0:T(1024)}, f32[8192]{0:T(1024)S(1)}, u32[]{:S(2)}) copy-start(f32[8192]{0:T(1024)S(1)} %get-tuple-element.36) | copy-start | bytes 98308
  623.0 235.4 %all-to-all-start.2 = ((bf16[32,640,512]{2,1,0:T(8,128)(2,1)}), bf16[32,640,512]{2,1,0:T(8,128)(2,1)}, u32[]{:S(2)}, u32[]{:S(2)}) async-start(bf16[32,640,512]{2,1,0:T(8,128)(2,1)} %bitcast.130), calls=%async_computation.2 | async-start | bytes 41943040 | tf_op jit(solution)/shard_map/all_to_all | solution.py:92
  630.7 1411.8 %all-reduce.7.cloned.1.call-start = ((), (), s32[]{:S(2)}) async-start(), calls=%async_computation.5 | async-start | bytes 83886080 | tf_op jit(solution)/shard_map/psum | solution.py:83
  2283.1 8.6 copy-start.4
  2283.1 8.6 copy-start.12
  2283.1 235.5 %all-to-all-start.3 = ((bf16[32,640,512]{2,1,0:T(8,128)(2,1)}), bf16[32,640,512]{2,1,0:T(8,128)(2,1)}, u32[]{:S(2)}, u32[]{:S(2)}) async-start(bf16[32,640,512]{2,1,0:T(8,128)(2,1)} %get-tuple-element.24), calls=%async_computation.3 | async-start | bytes 41943040 | tf_op jit(solution)/shard_map/all_to_all | solution.py:101
  2291.0 377.1 %all-reduce.5.cloned.1.call-start = ((), (), s32[]{:S(2)}) async-start(), calls=%async_computation.4 | async-start | bytes 131072 | tf_op jit(solution)/shard_map/psum | solution.py:109
  2562.1 43.4 %copy-start.10 = (f32[8192]{0:T(1024)S(1)}, f32[8192]{0:T(1024)}, u32[]{:S(2)}) copy-start(f32[8192]{0:T(1024)} %copy-done.9) | copy-start | bytes 98308
  2562.1 43.4 %copy-start.16 = (f32[8192]{0:T(1024)S(1)}, f32[8192]{0:T(1024)}, u32[]{:S(2)}) copy-start(f32[8192]{0:T(1024)} %copy-done.15) | copy-start | bytes 98308
  2562.1 43.5 %copy-start.22 = (pred[8192]{0:T(1024)(128)(4,1)S(1)}, pred[8192]{0:T(1024)(128)(4,1)}, u32[]{:S(2)}) copy-start(pred[8192]{0:T(1024)(128)(4,1)} %get-tuple-element.42) | copy-start | bytes 24580
  2562.1 43.5 %copy-start.23 = (pred[8192]{0:T(1024)(128)(4,1)S(1)}, pred[8192]{0:T(1024)(128)(4,1)}, u32[]{:S(2)}) copy-start(pred[8192]{0:T(1024)(128)(4,1)} %get-tuple-element.43) | copy-start | bytes 24580
  2605.5 15.8 copy-start.2
  2605.6 15.8 copy-start.5
  2605.6 15.8 copy-start.8
  2605.6 15.8 copy-start.19
  2605.6 15.8 copy-start.24
  2605.6 15.8 copy-start.25
  2605.6 15.8 copy-start.30
  2605.6 21.3 copy-start.21
  2605.6 21.3 copy-start.27
  2626.9 17.5 copy-start.28
  2627.0 23.8 copy-start.32
  (6 other events, 37.5 us)
Sparse Core Ops, SparseCore 0:
  1129.2 913.3 all-reduce.6
  2627.0 25.8 all-reduce.4
where the time goes:
time: 2690 us; the launch traced here: 2680 us
  waiting for transfers between devices  1100 us (41%)
  local copies, waits for them, and re-layouts  510 us (19%)
  blocking collectives  476 us (18%)
  matrix products  446 us (17%)
  other arithmetic  106 us (4%)
    psum x1, waiting for transfers between devices, device_block(): exp_out = lax.psum(part_out, 'tp')  914 us
    gather x6, local copies, waits for them, and re-layouts, pick_rows(): return jnp.take(row_data, slot_index, axis=0, mode='fill', fill_value=0)  349 us
    all_to_all x1, blocking collectives, device_block(): lax.all_to_all(exp_out.reshape(experts, slot_cap, model_width), 'ep', 0,...  241 us
    psum x1, blocking collectives, device_block(): first_count = lax.psum(jnp.sum(one_first, axis=0), 'ep')  229 us
    all_to_all x1, waiting for transfers between devices, device_block(): lax.all_to_all(do_slot.reshape(experts, slot_cap, model_width), 'ep', 0,...  145 us
    dot_general x1, matrix products, device_block(): jnp.einsum('sxcd,xfd->sxcf', do_recv, out_loc, preferred_element_type=jnp...  124 us
    scatter x2, local copies, waits for them, and re-layouts, slot_tables(): slot_tok = slot_tok.at[slot_first].set(tok_ids).at[slot_second].set(tok_ids)  61 us
    scatter x2, local copies, waits for them, and re-layouts, slot_tables(): slot_gate.at[slot_first].set(gate_first).at[slot_second].set(gate_second)  61 us
  transfers between devices with their start and end apart: 5, of which 3 were waited for; matrix products, arithmetic and copies ran while one was open for 18% of the time, Pallas kernels for 0%

commit v1 on v0

v1 whole, which is shorter than its diff:
```python
import functools

import jax
import jax.numpy as jnp
from jax import lax
from jax.experimental import pallas as pl
from jax.experimental.pallas import tpu as pltpu
from jax.sharding import PartitionSpec as P


NORM_EPS = 1e-6
Z_COEF = 0.001
AUX_COEF = 0.01
GELU_C = 0.7978845608028654
GELU_A = 0.044715
LANES = 128
VMEM_LIMIT = 64 * 1024 * 1024 - 128 * 1024


def row_gather_kernel(split, blocks, tok_ref, side_ref, x_ref, dya_ref, dyb_ref, scale_ref, gate_ref,
                      u_ref, do_ref, table, rows_buf):
    step = pl.program_id(0)
    tok_block, width = x_ref.shape
    slices = width // LANES
    tile = 2 * slices
    slot_cap = u_ref.shape[1]

    @pl.when(step < blocks)
    def _():
        x_wide = x_ref[...].astype(jnp.float32)
        inv_rms = lax.rsqrt(jnp.mean(x_wide * x_wide, axis=-1, keepdims=True) + NORM_EPS)
        u_wide = (x_wide * inv_rms * scale_ref[...]).astype(jnp.bfloat16).astype(jnp.float32)
        if split:
            half = blocks // 2
            dy_val = jnp.where(step // half == side_ref[0], dya_ref[...], dyb_ref[...]).astype(jnp.float32)
        else:
            dy_val = dya_ref[...].astype(jnp.float32)
        base = pl.multiple_of(step * (tok_block * tile), tile)
        for k in range(slices):
            cols = slice(k * LANES, (k + 1) * LANES)
            table[pl.ds(base + k, tok_block, stride=tile), :] = u_wide[:, cols]
            table[pl.ds(base + slices + k, tok_block, stride=tile), :] = dy_val[:, cols]

    @pl.when(step == 0)
    def _():
        table[pl.ds(blocks * tok_block * tile, tile), :] = jnp.zeros((tile, LANES), jnp.float32)

    @pl.when(step >= blocks)
    def _():
        first = (step - blocks) * slot_cap
        unroll = 16 if slot_cap % 16 == 0 else 1

        def body(i, carry):
            for q in range(unroll):
                slot = i * unroll + q
                tok = tok_ref[first + slot]
                rows_buf[pl.ds(pl.multiple_of(slot * tile, tile), tile), :] = \
                    table[pl.ds(pl.multiple_of(tok * tile, tile), tile), :]
            return carry

        lax.fori_loop(0, slot_cap // unroll, body, 0)
        gate = gate_ref[0]
        for k in range(slices):
            cols = slice(k * LANES, (k + 1) * LANES)
            u_ref[0, :, cols] = rows_buf[pl.ds(k, slot_cap, stride=tile), :].astype(jnp.bfloat16)
            dy_rows = rows_buf[pl.ds(slices + k, slot_cap, stride=tile), :]
            do_ref[0, :, cols] = (dy_rows * gate).astype(jnp.bfloat16)


def gather_rows(slot_tok, side, x_grp, dy_parts, scale_row, gate_col):
    tok_count, width = x_grp.shape
    local_exp, slot_cap, _ = gate_col.shape
    tok_block = 512
    blocks = tok_count // tok_block
    half = blocks // 2
    tile = 2 * width // LANES
    split = len(dy_parts) == 2
    if split:
        dya, dyb = dy_parts
        map_a = lambda i, tok, sd: (jnp.clip(i - sd[0] * half, 0, half - 1), 0)
        map_b = lambda i, tok, sd: (jnp.clip(i - (1 - sd[0]) * half, 0, half - 1), 0)
    else:
        dya = dyb = dy_parts[0]
        map_a = lambda i, tok, sd: (jnp.minimum(i, blocks - 1), 0)
        map_b = lambda i, tok, sd: (0, 0)
    exp_map = lambda i, tok, sd: (jnp.maximum(i - blocks, 0), 0, 0)
    tok_spec = (tok_block, width)
    row_shape = jax.ShapeDtypeStruct((local_exp, slot_cap, width), jnp.bfloat16)
    return pl.pallas_call(
        functools.partial(row_gather_kernel, split, blocks),
        grid_spec=pltpu.PrefetchScalarGridSpec(
            num_scalar_prefetch=2,
            grid=(blocks + local_exp,),
            in_specs=[
                pl.BlockSpec(tok_spec, lambda i, tok, sd: (jnp.minimum(i, blocks - 1), 0)),
                pl.BlockSpec(tok_spec, map_a),
                pl.BlockSpec(tok_spec, map_b),
                pl.BlockSpec((1, width), lambda i, tok, sd: (0, 0)),
                pl.BlockSpec((1, slot_cap, 1), exp_map),
            ],
            out_specs=[pl.BlockSpec((1, slot_cap, width), exp_map)] * 2,
            scratch_shapes=[
                pltpu.VMEM(((tok_count + 1) * tile, LANES), jnp.float32),
                pltpu.VMEM((slot_cap * tile, LANES), jnp.float32),
            ],
        ),
        out_shape=[row_shape, row_shape],
        compiler_params=pltpu.CompilerParams(vmem_limit_bytes=VMEM_LIMIT, dimension_semantics=("arbitrary",)),
        cost_estimate=pl.CostEstimate(flops=30_000_000_000, bytes_accessed=40_000_000, transcendentals=0),
        name="gather_rows",
    )(slot_tok, side, x_grp, dya, dyb, scale_row, gate_col)


def dot_nt(lhs, rhs):
    return lax.dot_general(lhs, rhs, (((1,), (1,)), ((), ())), preferred_element_type=jnp.float32)


def dot_tn(lhs, rhs):
    return lax.dot_general(lhs, rhs, (((0,), (0,)), ((), ())), preferred_element_type=jnp.float32)


def dot_nn(lhs, rhs):
    return jnp.dot(lhs, rhs, preferred_element_type=jnp.float32)


def expert_kernel(side_ref, u_ref, do_ref, gate_ref, lin_ref, out_ref,
                  o_keep, o_send, du_keep, du_send, h_ref, da0_ref, da1_ref):
    width = u_ref.shape[2]
    ff = gate_ref.shape[2]
    chunk = 256
    u_rows = u_ref[0]
    do_rows = do_ref[0]
    o_acc = None
    du_acc = None
    for f in range(0, ff, chunk):
        cols = slice(f, f + chunk)
        a0 = dot_nn(u_rows, gate_ref[0, :, cols])
        a1 = dot_nn(u_rows, lin_ref[0, :, cols])
        dh = dot_nt(do_rows, out_ref[0, cols, :])
        sq = a0 * a0
        th = jnp.tanh(GELU_C * (a0 + GELU_A * (sq * a0)))
        cdf = 0.5 * (1.0 + th)
        gelu = a0 * cdf
        slope = cdf + (0.5 * GELU_C) * a0 * (1.0 - th * th) * (1.0 + (3.0 * GELU_A) * sq)
        h = (gelu * a1).astype(jnp.bfloat16)
        da0 = (dh * a1 * slope).astype(jnp.bfloat16)
        da1 = (dh * gelu).astype(jnp.bfloat16)
        h_ref[0, :, cols] = h
        da0_ref[0, :, cols] = da0
        da1_ref[0, :, cols] = da1
        o_part = dot_nn(h, out_ref[0, cols, :])
        du_part = dot_nt(da0, gate_ref[0, :, cols]) + dot_nt(da1, lin_ref[0, :, cols])
        o_acc = o_part if o_acc is None else o_acc + o_part
        du_acc = du_part if du_acc is None else du_acc + du_part
    half = width // 2
    low_side = side_ref[0] == 0
    for acc, keep, send in ((o_acc, o_keep, o_send), (du_acc, du_keep, du_send)):
        low = acc[:, :half].astype(jnp.bfloat16)
        high = acc[:, half:].astype(jnp.bfloat16)
        keep[0] = jnp.where(low_side, low, high)
        send[0] = jnp.where(low_side, high, low)


def run_experts(side, u_rows, do_rows, gate_loc, lin_loc, out_loc):
    local_exp, slot_cap, width = u_rows.shape
    ff = gate_loc.shape[2]
    exp_map = lambda e, sd: (e, 0, 0)
    row_block = pl.BlockSpec((1, slot_cap, width), exp_map)
    in_block = pl.BlockSpec((1, width, ff), exp_map)
    out_block = pl.BlockSpec((1, ff, width), exp_map)
    half_block = pl.BlockSpec((1, slot_cap, width // 2), exp_map)
    ff_block = pl.BlockSpec((1, slot_cap, ff), exp_map)
    half_shape = jax.ShapeDtypeStruct((local_exp, slot_cap, width // 2), jnp.bfloat16)
    ff_shape = jax.ShapeDtypeStruct((local_exp, slot_cap, ff), jnp.bfloat16)
    return pl.pallas_call(
        expert_kernel,
        grid_spec=pltpu.PrefetchScalarGridSpec(
            num_scalar_prefetch=1,
            grid=(local_exp,),
            in_specs=[row_block, row_block, in_block, in_block, out_block],
            out_specs=[half_block] * 4 + [ff_block] * 3,
        ),
        out_shape=[half_shape] * 4 + [ff_shape] * 3,
        compiler_params=pltpu.CompilerParams(vmem_limit_bytes=VMEM_LIMIT, dimension_semantics=("arbitrary",)),
        cost_estimate=pl.CostEstimate(flops=60_000_000_000, bytes_accessed=100_000_000, transcendentals=0),
        name="expert_pass",
    )(side, u_rows, do_rows, gate_loc, lin_loc, out_loc)


def weight_grad_kernel(groups, *refs):
    ins, (dg_ref, dl_ref, dw_ref) = refs[:5 * groups], refs[5 * groups:]
    d_gate = d_lin = d_out = None
    for g in range(groups):
        u_ref, do_ref, h_ref, da0_ref, da1_ref = ins[5 * g:5 * g + 5]
        pg = dot_tn(u_ref[0], da0_ref[0])
        pn = dot_tn(u_ref[0], da1_ref[0])
        po = dot_tn(h_ref[0], do_ref[0])
        d_gate = pg if d_gate is None else d_gate + pg
        d_lin = pn if d_lin is None else d_lin + pn
        d_out = po if d_out is None else d_out + po
    dg_ref[0] = d_gate
    dl_ref[0] = d_lin
    dw_ref[0] = d_out


def weight_grads(parts):
    local_exp, slot_cap, width = parts[0][0].shape
    ff = parts[0][2].shape[2]
    splits = 2
    ff_blk = ff // splits
    row_block = pl.BlockSpec((1, slot_cap, width), lambda e, f: (e, 0, 0))
    ff_block = pl.BlockSpec((1, slot_cap, ff_blk), lambda e, f: (e, 0, f))
    in_shape = jax.ShapeDtypeStruct((local_exp, width, ff), jnp.float32)
    out_shape = jax.ShapeDtypeStruct((local_exp, ff, width), jnp.float32)
    return pl.pallas_call(
        functools.partial(weight_grad_kernel, len(parts)),
        grid=(local_exp, splits),
        in_specs=[row_block, row_block, ff_block, ff_block, ff_block] * len(parts),
        out_specs=[pl.BlockSpec((1, width, ff_blk), lambda e, f: (e, 0, f)),
                   pl.BlockSpec((1, width, ff_blk), lambda e, f: (e, 0, f)),
                   pl.BlockSpec((1, ff_blk, width), lambda e, f: (e, f, 0))],
        out_shape=[in_shape, in_shape, out_shape],
        compiler_params=pltpu.CompilerParams(vmem_limit_bytes=VMEM_LIMIT,
                                             dimension_semantics=("arbitrary", "arbitrary")),
        cost_estimate=pl.CostEstimate(flops=80_000_000_000, bytes_accessed=250_000_000, transcendentals=0),
        name="weight_grads",
    )(*[a for part in parts for a in part])


def rows_to_cols(rows):
    return jnp.transpose(rows, (1, 0))


def lane_pack(cols, lanes=LANES):
    count = cols[0].shape[0]
    lane = lax.broadcasted_iota(jnp.int32, (count, lanes), 1)
    packed = jnp.zeros((count, lanes), jnp.float32)
    for i, col in enumerate(cols):
        packed = jnp.where(lane == i, col, packed)
    return jnp.transpose(packed, (1, 0))[:8]


def fill_table(step, steps_each, sources, table):
    blk, slot_cap, half = sources[0].shape
    slices = half // LANES
    for g, src in enumerate(sources):
        @pl.when(step // steps_each == g)
        def _():
            rows = blk * slot_cap
            vals = src[...].reshape(rows, half).astype(jnp.float32)
            base = pl.multiple_of(step * (rows * slices), 8)
            for k in range(slices):
                table[pl.ds(base + k, rows, stride=slices), :] = vals[:, k * LANES:(k + 1) * LANES]


def pick_table(table, buf, row_ref, first, count, slices):
    unroll = 16

    def body(i, carry):
        for q in range(unroll):
            tok = i * unroll + q
            buf[pl.ds(pl.multiple_of(tok * slices, slices), slices), :] = \
                table[pl.ds(pl.multiple_of(row_ref[first + tok] * slices, slices), slices), :]
        return carry

    lax.fori_loop(0, count // unroll, body, 0)


def buf_slice(buf, k, count, slices):
    return buf[pl.ds(k, count, stride=slices), :]


def combine_o_kernel(table_steps, groups, row1_ref, row2_ref, side_ref, *refs):
    sources, (x_ref, dy_ref, feat_ref, y_ref, part_ref, table, buf1, buf2) = refs[:groups], refs[groups:]
    step = pl.program_id(0)
    count, half = x_ref.shape
    slices = half // LANES

    @pl.when(step == 0)
    def _():
        zero_at = table.shape[0] - 8
        table[pl.ds(zero_at, 8), :] = jnp.zeros((8, LANES), jnp.float32)

    @pl.when(step < table_steps)
    def _():
        fill_table(step, table_steps // groups, sources, table)

    @pl.when(step >= table_steps)
    def _():
        first = (step - table_steps) * count
        pick_table(table, buf1, row1_ref, first, count, slices)
        pick_table(table, buf2, row2_ref, first, count, slices)
        feat = rows_to_cols(feat_ref[...])
        n1, n2 = feat[:, 0:1], feat[:, 1:2]
        dn1 = dn2 = 0.0
        for k in range(slices):
            cols = slice(k * LANES, (k + 1) * LANES)
            o1 = buf_slice(buf1, k, count, slices)
            o2 = buf_slice(buf2, k, count, slices)
            dy = dy_ref[:, cols].astype(jnp.float32)
            y_ref[:, cols] = (x_ref[:, cols].astype(jnp.float32) + n1 * o1 + n2 * o2).astype(jnp.bfloat16)
            dn1 = dn1 + dy * o1
            dn2 = dn2 + dy * o2
        part_ref[...] = lane_pack([jnp.sum(dn1, axis=-1, keepdims=True), jnp.sum(dn2, axis=-1, keepdims=True)])


def combine_du_kernel(table_steps, groups, row1_ref, row2_ref, side_ref, *refs):
    sources = refs[:groups]
    (x_ref, feat_ref, dl_ref, wr_ref, scale_ref, du_ref, part_ref, dr_ref, ds_ref, table, buf1, buf2) = refs[groups:]
    step = pl.program_id(0)
    count, half = x_ref.shape
    slices = half // LANES

    @pl.when(step == 0)
    def _():
        zero_at = table.shape[0] - 8
        table[pl.ds(zero_at, 8), :] = jnp.zeros((8, LANES), jnp.float32)
        dr_ref[...] = jnp.zeros_like(dr_ref)
        ds_ref[...] = jnp.zeros_like(ds_ref)

    @pl.when(step < table_steps)
    def _():
        fill_table(step, table_steps // groups, sources, table)

    @pl.when(step >= table_steps)
    def _():
        first = (step - table_steps) * count
        pick_table(table, buf1, row1_ref, first, count, slices)
        pick_table(table, buf2, row2_ref, first, count, slices)
        inv_rms = rows_to_cols(feat_ref[...])[:, 2:3]
        d_logits = dl_ref[...]
        routed = lax.dot_general(d_logits, wr_ref[...], (((0,), (0,)), ((), ())), preferred_element_type=jnp.float32)
        dot = 0.0
        norm_in = []
        for k in range(slices):
            cols = slice(k * LANES, (k + 1) * LANES)
            du_exp = buf_slice(buf1, k, count, slices) + buf_slice(buf2, k, count, slices)
            xn = x_ref[:, cols].astype(jnp.float32) * inv_rms
            scaled = xn * scale_ref[:, cols]
            du_all = du_exp + routed[:, cols]
            du_ref[:, cols] = du_all
            dot = dot + du_all * scaled
            ds_ref[:, cols] += jnp.sum(du_all * xn, axis=0, keepdims=True)
            norm_in.append(scaled.astype(jnp.bfloat16).astype(jnp.float32))
        part_ref[...] = lane_pack([jnp.sum(dot, axis=-1, keepdims=True)])
        dr_ref[...] += jnp.dot(d_logits, jnp.concatenate(norm_in, axis=1), preferred_element_type=jnp.float32)


def finish_dx_kernel(side_ref, du_ref, x_ref, dy_ref, feat_ref, part_a_ref, part_b_ref, scale_ref, dx_ref):
    width = 2 * x_ref.shape[1]
    inv_rms = rows_to_cols(feat_ref[...])[:, 2:3]
    mean = rows_to_cols(part_a_ref[...] + part_b_ref[...])[:, 0:1] * (1.0 / width)
    xn = x_ref[...].astype(jnp.float32) * inv_rms
    grad = dy_ref[...].astype(jnp.float32) + inv_rms * (du_ref[...] * scale_ref[...] - xn * mean)
    dx_ref[...] = grad.astype(jnp.bfloat16)


TOK_BLOCK = 512


def half_specs(offset):
    at = lambda i: jnp.maximum(i - offset, 0)
    tok = lambda i, r1, r2, sd: (at(i), 0)
    half_tok = lambda i, r1, r2, sd: (at(i), sd[0])
    row = lambda i, r1, r2, sd: (0, at(i))
    return tok, half_tok, row


def combine_call(kernel, rows, side, sources, extra, extra_specs, outs, out_specs, tok_count):
    local_exp, slot_cap, half = sources[0].shape
    groups = len(sources)
    blk = 2
    each = local_exp // blk
    table_steps = groups * each
    slices = half // LANES
    src_specs = [pl.BlockSpec((blk, slot_cap, half), (lambda g: lambda i, r1, r2, sd: (jnp.clip(i - g * each, 0, each - 1), 0, 0))(g))
                 for g in range(groups)]
    return pl.pallas_call(
        functools.partial(kernel, table_steps, groups),
        grid_spec=pltpu.PrefetchScalarGridSpec(
            num_scalar_prefetch=3,
            grid=(table_steps + tok_count // TOK_BLOCK,),
            in_specs=src_specs + extra_specs(table_steps),
            out_specs=out_specs(table_steps),
            scratch_shapes=[
                pltpu.VMEM((groups * local_exp * slot_cap * slices + 8, LANES), jnp.float32),
                pltpu.VMEM((TOK_BLOCK * slices, LANES), jnp.float32),
                pltpu.VMEM((TOK_BLOCK * slices, LANES), jnp.float32),
            ],
        ),
        out_shape=outs,
        compiler_params=pltpu.CompilerParams(vmem_limit_bytes=VMEM_LIMIT, dimension_semantics=("arbitrary",)),
        cost_estimate=pl.CostEstimate(flops=50_000_000_000, bytes_accessed=40_000_000, transcendentals=0),
    )(rows[0], rows[1], side, *sources, *extra)


def combine_o(rows, side, sources, x_loc, dy_loc, feat):
    tok_count, width = x_loc.shape
    half = width // 2

    def ins(offset):
        _, half_tok, row = half_specs(offset)
        return [pl.BlockSpec((TOK_BLOCK, half), half_tok)] * 2 + [pl.BlockSpec((8, TOK_BLOCK), row)]

    def out_specs(offset):
        tok, _, row = half_specs(offset)
        return [pl.BlockSpec((TOK_BLOCK, half), tok), pl.BlockSpec((8, TOK_BLOCK), row)]

    outs = [jax.ShapeDtypeStruct((tok_count, half), jnp.bfloat16), jax.ShapeDtypeStruct((8, tok_count), jnp.float32)]
    return combine_call(combine_o_kernel, rows, side, sources, (x_loc, dy_loc, feat), ins, outs, out_specs, tok_count)


def combine_du(rows, side, sources, x_loc, feat, d_logits_t, router_half_t, scale_half):
    tok_count, width = x_loc.shape
    half = width // 2
    experts = d_logits_t.shape[0]
    whole = lambda i, r1, r2, sd: (0, 0)

    def ins(offset):
        _, half_tok, row = half_specs(offset)
        return [pl.BlockSpec((TOK_BLOCK, half), half_tok), pl.BlockSpec((8, TOK_BLOCK), row),
                pl.BlockSpec((experts, TOK_BLOCK), row), pl.BlockSpec((experts, half), whole),
                pl.BlockSpec((1, half), whole)]

    def out_specs(offset):
        tok, _, row = half_specs(offset)
        return [pl.BlockSpec((TOK_BLOCK, half), tok), pl.BlockSpec((8, TOK_BLOCK), row),
                pl.BlockSpec((experts, half), whole), pl.BlockSpec((1, half), whole)]

    outs = [jax.ShapeDtypeStruct((tok_count, half), jnp.float32), jax.ShapeDtypeStruct((8, tok_count), jnp.float32),
            jax.ShapeDtypeStruct((experts, half), jnp.float32), jax.ShapeDtypeStruct((1, half), jnp.float32)]
    return combine_call(combine_du_kernel, rows, side, sources,
                        (x_loc, feat, d_logits_t, router_half_t, scale_half), ins, outs, out_specs, tok_count)


def finish_dx(side, du_all, x_loc, dy_loc, feat, part_a, part_b, scale_half):
    tok_count, half = du_all.shape
    tok = lambda i, sd: (i, 0)
    half_tok = lambda i, sd: (i, sd[0])
    row = lambda i, sd: (0, i)
    return pl.pallas_call(
        finish_dx_kernel,
        grid_spec=pltpu.PrefetchScalarGridSpec(
            num_scalar_prefetch=1,
            grid=(tok_count // TOK_BLOCK,),
            in_specs=[pl.BlockSpec((TOK_BLOCK, half), tok), pl.BlockSpec((TOK_BLOCK, half), half_tok),
                      pl.BlockSpec((TOK_BLOCK, half), half_tok)] + [pl.BlockSpec((8, TOK_BLOCK), row)] * 3 +
                     [pl.BlockSpec((1, half), lambda i, sd: (0, 0))],
            out_specs=pl.BlockSpec((TOK_BLOCK, half), tok),
        ),
        out_shape=jax.ShapeDtypeStruct((tok_count, half), jnp.bfloat16),
        compiler_params=pltpu.CompilerParams(vmem_limit_bytes=VMEM_LIMIT, dimension_semantics=("arbitrary",)),
        cost_estimate=pl.CostEstimate(flops=10_000_000_000, bytes_accessed=20_000_000, transcendentals=0),
        name="finish_dx",
    )(side, du_all, x_loc, dy_loc, feat, part_a, part_b, scale_half)


def slot_positions(hit_first, hit_second):
    rank_first = jnp.cumsum(hit_first, axis=0) - hit_first
    rank_second = jnp.cumsum(hit_second, axis=0) - hit_second + jnp.sum(hit_first, axis=0)
    return jnp.sum(rank_first * hit_first, axis=1), jnp.sum(rank_second * hit_second, axis=1)


def round_bf16(val):
    return lax.reduce_precision(val, 8, 7)


def solution(mesh):
    ep_size = mesh.shape['ep']
    tp_size = mesh.shape['tp']

    def swap_ep(val, bit):
        return lax.ppermute(val, 'ep', [(i, i ^ bit) for i in range(ep_size)])

    def swap_tp(val):
        return lax.ppermute(val, 'tp', [(i, i ^ 1) for i in range(tp_size)])

    def device_body(x_loc, dy_loc, idx_loc, norm_scale, w_router, gate_loc, lin_loc, out_loc):
        tok_count, width = x_loc.shape
        experts = w_router.shape[1]
        local_exp = gate_loc.shape[0]
        tokens = tok_count * ep_size
        slot_cap = (5 * tok_count + 2 * experts - 1) // (2 * experts)
        half = width // 2
        me = lax.axis_index('ep')
        side = lax.axis_index('tp')
        side_arr = side.astype(jnp.int32).reshape(1)

        dy_half = lax.dynamic_slice_in_dim(dy_loc, side * (tok_count // 2), tok_count // 2, axis=0)
        dy2_a = swap_ep(dy_half, 2)
        x2 = swap_ep(x_loc, 2)
        dy2_b = swap_tp(dy2_a)
        x1 = swap_ep(x_loc, 1)
        dy1 = swap_ep(dy_loc, 1)
        x3 = swap_ep(x2, 1)
        dy3_a = swap_ep(dy2_a, 1)
        dy3_b = swap_ep(dy2_b, 1)
        x_grp = (x_loc, x1, x2, x3)
        dy_grp = ((dy_loc,), (dy1,), (dy2_a, dy2_b), (dy3_a, dy3_b))

        x_wide = x_loc.astype(jnp.float32)
        inv_rms = lax.rsqrt(jnp.mean(x_wide * x_wide, axis=-1, keepdims=True) + NORM_EPS)
        u_tok = (x_wide * inv_rms * norm_scale).astype(jnp.bfloat16)
        u_wide = u_tok.astype(jnp.float32)
        logits = jnp.dot(u_wide, w_router, preferred_element_type=jnp.float32)
        log_norm = jax.nn.logsumexp(logits, axis=-1)
        router_prob = jnp.exp(logits - log_norm[:, None])
        expert_ids = jnp.arange(experts, dtype=jnp.int32)
        hit_first = idx_loc[:, 0:1] == expert_ids
        hit_second = idx_loc[:, 1:2] == expert_ids
        one_first = hit_first.astype(jnp.float32)
        one_second = hit_second.astype(jnp.float32)
        gate_first = jnp.sum(router_prob * one_first, axis=-1)
        gate_second = jnp.sum(router_prob * one_second, axis=-1)
        gate_total = gate_first + gate_second
        norm_first = gate_first / gate_total
        norm_second = gate_second / gate_total

        pos_first, pos_second = slot_positions(hit_first.astype(jnp.int32), hit_second.astype(jnp.int32))
        tok_ids = jnp.arange(tok_count, dtype=jnp.int32)
        tok_hi = (tok_ids // 64).astype(jnp.float32)
        tok_lo = (tok_ids % 64).astype(jnp.float32)
        slot_ids = jnp.arange(slot_cap, dtype=jnp.int32)
        table = 0.0
        for one, pos, norm in ((one_first, pos_first, norm_first), (one_second, pos_second, norm_second)):
            g_hi = round_bf16(norm)
            g_mid = round_bf16(norm - g_hi)
            g_lo = round_bf16(norm - g_hi - g_mid)
            feats = [jnp.ones_like(norm), tok_hi, tok_lo, g_hi, g_mid, g_lo]
            left = jnp.concatenate([one * f[:, None] for f in feats], axis=1).astype(jnp.bfloat16)
            right = (pos[:, None] == slot_ids).astype(jnp.bfloat16)
            table = table + lax.dot_general(left, right, (((0,), (0,)), ((), ())), preferred_element_type=jnp.float32)
        table = table.reshape(6, experts, slot_cap)
        slot_tok = jnp.where(table[0] > 0.5, table[1] * 64.0 + table[2], float(tok_count))
        slot_gate = table[3] + table[4] + table[5]
        slot_pack = jnp.stack([slot_tok, slot_gate]).reshape(2, ep_size, local_exp, slot_cap)

        scale_row = norm_scale.reshape(1, width)
        saved = {}
        back_o = [None] * ep_size
        back_du = [None] * ep_size
        sent = {}
        for bit in range(ep_size):
            pack = lax.dynamic_index_in_dim(slot_pack, me ^ bit, axis=1, keepdims=False)
            if bit:
                pack = swap_ep(pack, bit)
            tok_grp = pack[0].astype(jnp.int32).reshape(local_exp * slot_cap)
            gate_grp = pack[1].reshape(local_exp, slot_cap, 1)
            u_rows, do_rows = gather_rows(tok_grp, side_arr, x_grp[bit], dy_grp[bit], scale_row, gate_grp)
            o_keep, o_send, du_keep, du_send, h, da0, da1 = run_experts(
                side_arr, u_rows, do_rows, gate_loc, lin_loc, out_loc)
            saved[bit] = (u_rows, do_rows, h, da0, da1)
            sent[bit] = (o_keep, o_send, du_keep, du_send)
        for bit in range(ep_size):
            o_keep, o_send, du_keep, du_send = sent[bit]
            o_got = swap_tp(o_send)
            du_got = swap_tp(du_send)
            o_sum = (o_keep.astype(jnp.float32) + o_got.astype(jnp.float32)).astype(jnp.bfloat16)
            du_sum = (du_keep.astype(jnp.float32) + du_got.astype(jnp.float32)).astype(jnp.bfloat16)
            if bit:
                o_sum = swap_ep(o_sum, bit)
                du_sum = swap_ep(du_sum, bit)
            back_o[bit] = o_sum
            back_du[bit] = du_sum
        d_gate, d_lin, d_out = weight_grads([saved[b] for b in range(ep_size)])

        per_dev = local_exp * slot_cap

        def slot_row(exp_idx, pos):
            row = ((exp_idx // local_exp) ^ me) * per_dev + (exp_idx % local_exp) * slot_cap + pos
            return jnp.where(pos < slot_cap, row, ep_size * per_dev)

        rows = (slot_row(idx_loc[:, 0], pos_first), slot_row(idx_loc[:, 1], pos_second))
        half_of = lambda val, axis: lax.dynamic_slice_in_dim(val, side * half, half, axis=axis)
        scale_half = half_of(norm_scale, 0)[None, :]
        zero_row = jnp.zeros_like(norm_first)
        feat = jnp.stack([norm_first, norm_second, inv_rms[:, 0]] + [zero_row] * 5)
        y_half, part_o = combine_o(rows, side_arr, back_o, x_loc, dy_loc, feat)
        y_other = swap_tp(y_half)
        part_o = part_o + swap_tp(part_o)
        dn_first, dn_second = part_o[0], part_o[1]

        stats = jnp.concatenate([jnp.sum(one_first, axis=0), jnp.sum(router_prob, axis=0),
                                 jnp.sum(log_norm * log_norm).reshape(1)])
        stats = lax.psum(stats, 'ep')
        first_count, prob_sum, norm_sq = stats[:experts], stats[experts:2 * experts], stats[2 * experts]
        frac_first = first_count / tokens
        z_loss = Z_COEF * norm_sq / tokens
        aux_loss = AUX_COEF * experts * jnp.sum(frac_first * prob_sum) / tokens
        gate_mix = norm_first * dn_first + norm_second * dn_second
        aux_coef = AUX_COEF * experts * frac_first
        d_logits = router_prob * (aux_coef - jnp.sum(aux_coef * router_prob, axis=-1, keepdims=True))
        d_logits = d_logits + (2.0 * Z_COEF) * log_norm[:, None] * router_prob
        d_logits = d_logits + one_first * (norm_first * (dn_first - gate_mix))[:, None]
        d_logits = d_logits + one_second * (norm_second * (dn_second - gate_mix))[:, None]

        du_all, part_du, d_router_half, d_scale_half = combine_du(
            rows, side_arr, back_du, x_loc, feat, d_logits.T, half_of(w_router, 0).T, scale_half)
        part_other = swap_tp(part_du)
        dx_half = finish_dx(side_arr, du_all, x_loc, dy_loc, feat, part_du, part_other, scale_half)
        sums = jnp.concatenate([d_router_half, d_scale_half])
        dx_half, sums = lax.optimization_barrier((dx_half, sums))
        dx_other = swap_tp(dx_half)
        sums = lax.dynamic_update_slice_in_dim(jnp.zeros((experts + 1, width), jnp.float32), sums, side * half, axis=1)
        sums = lax.psum(sums, ('ep', 'tp'))
        d_router = sums[:experts].T
        d_scale = sums[experts]

        def join(mine, other):
            return jnp.where(side == 0, jnp.concatenate([mine, other], axis=1), jnp.concatenate([other, mine], axis=1))

        y_loc = join(y_half, y_other)
        dx_loc = join(dx_half, dx_other)
        losses = jnp.stack([z_loss, aux_loss])
        return (y_loc, losses, dx_loc, d_scale, d_router, d_gate, d_lin, d_out)

    tok_spec = P('ep', None)
    in_spec = P('ep', None, 'tp')
    out_spec = P('ep', 'tp', None)
    return jax.shard_map(device_body, mesh=mesh, in_specs=(tok_spec, tok_spec, tok_spec, P(), P(), in_spec, in_spec, out_spec), out_specs=(tok_spec, P(), tok_spec, P(), P(), in_spec, in_spec, out_spec), check_vma=False)
```

time: 2690 us -> 1280 us (0.48)
  waiting for transfers between devices: 1100 us -> 343 us
  Pallas kernels: 0 us -> 524 us
  local copies, waits for them, and re-layouts: 510 us -> 28.6 us
  matrix products: 446 us -> 13.3 us
  blocking collectives: 476 us -> 235 us
    psum x2 -> x1, waiting for transfers between devices: 914 us -> 0.02 us  [device_body(): sums = lax.psum(sums, ('ep', 'tp'))]
    pallas_call x0 -> x12, Pallas kernels: none -> 524 us  [the longest x4 195 us: run_experts(): pl.pallas_call(expert_kernel, grid_spec=pltpu.PrefetchScalarGridSpec(num_...]
    dot_general x12 -> x3, matrix products: 446 us -> 13.3 us  [the longest x2 10.4 us: device_body(): lax.dot_general(left, right, (((0,), (0,)), ((), ())), preferred_element_...]
    gather x6 -> x0, local copies, waits for them, and re-layouts: 349 us -> none  [pick_rows(): return jnp.take(row_data, slot_index, axis=0, mode='fill', fill_value=0)]
    ppermute x0 -> x29, waiting for transfers between devices: none -> 343 us  [the longest x13 283 us: swap_tp(): return lax.ppermute(val, 'tp', [(i, i ^ 1) for i in range(tp_size)])]
    all_to_all x1 -> x0, blocking collectives: 241 us -> none  [device_block(): lax.all_to_all(exp_out.reshape(experts, slot_cap, model_width), 'ep', 0,...]
    all_to_all x3 -> x0, waiting for transfers between devices: 185 us -> none  [the longest x1 145 us: device_block(): lax.all_to_all(do_slot.reshape(experts, slot_cap, model_width), 'ep', 0,...]
    scatter x4 -> x0, local copies, waits for them, and re-layouts: 122 us -> none  [the longest x2 61 us: slot_tables(): slot_tok = slot_tok.at[slot_first].set(tok_ids).at[slot_second].set(tok_ids)]
  transfers between devices with their start and end apart: 5 -> 30, of which waited for: 3 -> 10; matrix products, arithmetic and copies ran while one was open for 18% -> 10% of each run, Pallas kernels for 0% -> 37%
where the time goes in v1:
time: 1280 us; the launch traced here: 1270 us
  Pallas kernels  524 us (41%)
  waiting for transfers between devices  343 us (27%)
  blocking collectives  235 us (18%)
  other arithmetic  92.6 us (7%)
  local copies, waits for them, and re-layouts  28.6 us (2%)
  starting transfers between devices  19.3 us (2%)
  between operations  16.5 us (1%)
  matrix products  13.3 us (1%)
    ppermute x13, waiting for transfers between devices, swap_tp(): return lax.ppermute(val, 'tp', [(i, i ^ 1) for i in range(tp_size)])  283 us
    psum x1, blocking collectives, device_body(): stats = lax.psum(stats, 'ep')  235 us
    pallas_call x4, Pallas kernels, run_experts(): pl.pallas_call(expert_kernel, grid_spec=pltpu.PrefetchScalarGridSpec(num_...  195 us
    pallas_call x4, Pallas kernels, gather_rows(): pl.pallas_call(functools.partial(row_gather_kernel, split, blocks), grid_...  123 us
    pallas_call x2, Pallas kernels, combine_call(): pl.pallas_call(functools.partial(kernel, table_steps, groups), grid_spec=...  101 us
    pallas_call x1, Pallas kernels, weight_grads(): pl.pallas_call(functools.partial(weight_grad_kernel, len(parts)), grid=(l...  89.9 us
    ppermute x16, waiting for transfers between devices, swap_ep(): return lax.ppermute(val, 'ep', [(i, i ^ bit) for i in range(ep_size)])  60.5 us
  transfers between devices with their start and end apart: 30, of which 10 were waited for; matrix products, arithmetic and copies ran while one was open for 10% of the time, Pallas kernels for 37%

profile of v1, /device:TPU:0, one launch (start us, length us, event | category | flops | bytes accessed | tf_op | source)
XLA Modules:
  0.0 1273.2 jit_solution(2748281938063766987)
XLA Ops:
  10.8 4.8 constant_dynamic-slice_fusion
  24.8 9.5 reduce-window.14
  36.9 9.5 reduce-window.16
  49.5 235.2 %psum.14 = f32[65]{0:T(128)S(1)} all-reduce(f32[65]{0:T(128)S(1)} %pad_maximum_fusion.1), channel_id=1, replica_groups=mesh['tp'=2,'ep'=4] {'ep'}, use_global_device_ids=true, to_apply=%region_15.16 | all-reduce | flops 65 | bytes 520 | tf_op jit(solution)/shard_map/psum | solution.py:585
  291.8 6.2 fusion
  299.3 4.2 fusion.11
  307.1 30.9 %gather_rows.4 = (bf16[8,640,512]{2,1,0:T(8,128)(2,1)}, bf16[8,640,512]{2,1,0:T(8,128)(2,1)}) custom-call(s32[5120]{0:T(1024)} %convert_element_type.160.tok_ref, s32[1]{0:T(128)} %bitcast.6.side_ref, bf16[8192,512]{1,0:T(8,128)(2,1)} %x_ref.3, bf16[8192,512]{1,0:T(8,128)(2,1)} %dy_ref.1, bf16[8192,512]{1,0:T(8,128)(2,1)} %dy_ref.1, f32[1,512]{1,0:T(1,128)} %bitcast.115, ...), custom_call_target="tpu_custom_call" | custom-call | flops 30000001024 | bytes 40000000 | tf_op jit(solution)/shard_map/gather_rows/pallas_call | solution.py:89
  352.7 30.5 %gather_rows.5 = (bf16[8,640,512]{2,1,0:T(8,128)(2,1)}, bf16[8,640,512]{2,1,0:T(8,128)(2,1)}) custom-call(s32[5120]{0:T(1024)} %convert_element_type.165.tok_ref, s32[1]{0:T(128)} %bitcast.6.side_ref, bf16[8192,512]{1,0:T(8,128)(2,1)} %collective-permute-done.2.x_ref, bf16[8192,512]{1,0:T(8,128)(2,1)} %collective-permute-done.3.dya_ref.dyb_ref, ...), custom_call_target="tpu_custom_call" | custom-call | flops 30000001024 | bytes 40000000 | tf_op jit(solution)/shard_map/gather_rows/pallas_call | solution.py:89
  383.2 48.5 %expert_pass.5 = (bf16[8,640,256]{2,1,0:T(8,128)(2,1)}, bf16[8,640,256]{2,1,0:T(8,128)(2,1)}, bf16[8,640,256]{2,1,0:T(8,128)(2,1)}, bf16[8,640,256]{2,1,0:T(8,12...) custom-call(s32[1]{0:T(128)} %bitcast.6.side_ref, ...), custom_call_target="tpu_custom_call" | custom-call | flops 60000002048 | bytes 100000000 | tf_op jit(solution)/shard_map/expert_pass/pallas_call | solution.py:175
  432.1 12.5 collective-permute-done.9.dyb_ref
  444.6 30.8 %gather_rows.6 = (bf16[8,640,512]{2,1,0:T(8,128)(2,1)}, bf16[8,640,512]{2,1,0:T(8,128)(2,1)}) custom-call(s32[5120]{0:T(1024)} %convert_element_type.170.tok_ref, s32[1]{0:T(128)} %bitcast.6.side_ref, bf16[8192,512]{1,0:T(8,128)(2,1)} %collective-permute-done.7.x_ref, bf16[4096,512]{1,0:T(8,128)(2,1)} %collective-permute-done.8.dya_ref, ...), custom_call_target="tpu_custom_call" | custom-call | flops 30000001024 | bytes 40000000 | tf_op jit(solution)/shard_map/gather_rows/pallas_call | solution.py:89
  475.4 48.8 %expert_pass.6 = (bf16[8,640,256]{2,1,0:T(8,128)(2,1)}, bf16[8,640,256]{2,1,0:T(8,128)(2,1)}, bf16[8,640,256]{2,1,0:T(8,128)(2,1)}, bf16[8,640,256]{2,1,0:T(8,12...) custom-call(s32[1]{0:T(128)} %bitcast.6.side_ref, ...), custom_call_target="tpu_custom_call" | custom-call | flops 60000002048 | bytes 100000000 | tf_op jit(solution)/shard_map/expert_pass/pallas_call | solution.py:175
  525.7 30.7 %gather_rows.7 = (bf16[8,640,512]{2,1,0:T(8,128)(2,1)}, bf16[8,640,512]{2,1,0:T(8,128)(2,1)}) custom-call(s32[5120]{0:T(1024)} %convert_element_type.175.tok_ref, s32[1]{0:T(128)} %bitcast.6.side_ref, bf16[8192,512]{1,0:T(8,128)(2,1)} %collective-permute-done.13.x_ref, bf16[4096,512]{1,0:T(8,128)(2,1)} %collective-permute-done.14.dya_ref, ...), custom_call_target="tpu_custom_call" | custom-call | flops 30000001024 | bytes 40000000 | tf_op jit(solution)/shard_map/gather_rows/pallas_call | solution.py:89
  556.4 48.6 %expert_pass.7 = (bf16[8,640,256]{2,1,0:T(8,128)(2,1)}, bf16[8,640,256]{2,1,0:T(8,128)(2,1)}, bf16[8,640,256]{2,1,0:T(8,128)(2,1)}, bf16[8,640,256]{2,1,0:T(8,12...) custom-call(s32[1]{0:T(128)} %bitcast.6.side_ref, ...), custom_call_target="tpu_custom_call" | custom-call | flops 60000002048 | bytes 100000000 | tf_op jit(solution)/shard_map/expert_pass/pallas_call | solution.py:175
  605.6 48.8 %expert_pass.4 = (bf16[8,640,256]{2,1,0:T(8,128)(2,1)}, bf16[8,640,256]{2,1,0:T(8,128)(2,1)}, bf16[8,640,256]{2,1,0:T(8,128)(2,1)}, bf16[8,640,256]{2,1,0:T(8,12...) custom-call(s32[1]{0:T(128)} %bitcast.6.side_ref, ...), custom_call_target="tpu_custom_call" | custom-call | flops 60000002048 | bytes 100000000 | tf_op jit(solution)/shard_map/expert_pass/pallas_call | solution.py:175
  661.6 4.2 add_convert_fusion.5
  665.9 4.0 add_convert_fusion.4
  669.9 51.4 %collective-permute-done = bf16[8,640,256]{2,1,0:T(8,128)(2,1)} collective-permute-done((bf16[8,640,256]{2,1,0:T(8,128)(2,1)}, bf16[8,640,256]{2,1,0:T(8,128)(2,1)}, u32[]{:S(2)}, u32[]{:S(2)}) %collective-permute-start) | collective-permute-done | bytes 2621472 | tf_op jit(solution)/shard_map/ppermute | solution.py:476
  722.5 54.9 %collective-permute-done.19 = bf16[8,640,256]{2,1,0:T(8,128)(2,1)} collective-permute-done((bf16[8,640,256]{2,1,0:T(8,128)(2,1)}, bf16[8,640,256]{2,1,0:T(8,128)(2,1)}, u32[]{:S(2)}, u32[]{:S(2)}) %collective-permute-start.19) | collective-permute-done | bytes 2621472 | tf_op jit(solution)/shard_map/ppermute | solution.py:476
  781.1 4.6 add_convert_fusion.7.refs_0_
  785.7 4.1 add_convert_fusion.3.refs_0_
  789.9 43.8 %collective-permute-done.20 = bf16[8,640,256]{2,1,0:T(8,128)(2,1)} collective-permute-done((bf16[8,640,256]{2,1,0:T(8,128)(2,1)}, bf16[8,640,256]{2,1,0:T(8,128)(2,1)}, u32[]{:S(2)}, u32[]{:S(2)}) %collective-permute-start.20) | collective-permute-done | bytes 2621472 | tf_op jit(solution)/shard_map/ppermute | solution.py:476
  837.6 51.5 %collective-permute-done.22 = bf16[8,640,256]{2,1,0:T(8,128)(2,1)} collective-permute-done((bf16[8,640,256]{2,1,0:T(8,128)(2,1)}, bf16[8,640,256]{2,1,0:T(8,128)(2,1)}, u32[]{:S(2)}, u32[]{:S(2)}) %collective-permute-start.22) | collective-permute-done | bytes 2621472 | tf_op jit(solution)/shard_map/ppermute | solution.py:476
  894.4 50.5 %shard_map.143 = (bf16[8192,256]{1,0:T(8,128)(2,1)}, f32[8,8192]{1,0:T(8,128)}) custom-call(s32[8192]{0:T(1024)} %fusion.55.row1_ref, s32[8192]{0:T(1024)} %fusion.61.row2_ref, s32[1]{0:T(128)} %bitcast.6.side_ref, bf16[8,640,256]{2,1,0:T(8,128)(2,1)} %add_convert_fusion.7.refs_0_, bf16[8,640,256]{2,1,0:T(8,128)(2,1)} %collective-permute-done.5.refs_1_, ...), custom_call_target="tpu_custom_call" | custom-call | flops 49999998976 | bytes 40000000 | tf_op jit(solution)/shard_map/pallas_call | solution.py:378
  946.3 7.5 collective-permute-done.24
  958.9 57.2 %collective-permute-done.25.refs_3_ = bf16[8,640,256]{2,1,0:T(8,128)(2,1)S(1)} collective-permute-done((bf16[8,640,256]{2,1,0:T(8,128)(2,1)S(1)}, bf16[8,640,256]{2,1,0:T(8,128)(2,1)S(1)}, u32[]{:S(2)}, u32[]{:S(2)}) %collective-permute-start.25) | collective-permute-done | bytes 2621472 | tf_op jit(solution)/shard_map/ppermute | solution.py:473
  1017.6 50.4 %shard_map.144 = (f32[8192,256]{1,0:T(8,128)}, f32[8,8192]{1,0:T(8,128)}, f32[32,256]{1,0:T(8,128)}, f32[1,256]{1,0:T(1,128)}) custom-call(s32[8192]{0:T(1024)} %fusion.55.row1_ref, s32[8192]{0:T(1024)} %fusion.61.row2_ref, s32[1]{0:T(128)} %bitcast.6.side_ref, bf16[8,640,256]{2,1,0:T(8,128)(2,1)} %add_convert_fusion.3.refs_0_, ...), custom_call_target="tpu_custom_call" | custom-call | flops 49999998976 | bytes 40000000 | tf_op jit(solution)/shard_map/pallas_call | solution.py:378
  1077.6 16.1 %finish_dx.1 = bf16[8192,256]{1,0:T(8,128)(2,1)} custom-call(s32[1]{0:T(128)} %bitcast.6.side_ref, f32[8192,256]{1,0:T(8,128)} %get-tuple-element.81.du_ref, bf16[8192,512]{1,0:T(8,128)(2,1)} %x_ref.3, bf16[8192,512]{1,0:T(8,128)(2,1)} %dy_ref.1, f32[8,8192]{1,0:T(8,128)} %stack.22.refs_6_.refs_5_.feat_ref, f32[8,8192]{1,0:T(8,128)} %get-tuple-element.82.part_a_ref, ...), custom_call_target="tpu_custom_call" | custom-call | flops 10000000000 | bytes 20000000 | tf_op jit(solution)/shard_map/finish_dx/pallas_call | solution.py:441
  1095.7 89.9 %weight_grads.1 = (f32[8,512,1024]{2,1,0:T(8,128)}, f32[8,512,1024]{2,1,0:T(8,128)}, f32[8,1024,512]{2,1,0:T(8,128)}) custom-call(bf16[8,640,512]{2,1,0:T(8,128)(2,1)} %get-tuple-element.55.u_ref.refs_0_, bf16[8,640,512]{2,1,0:T(8,128)(2,1)} %get-tuple-element.56.do_ref.refs_1_, bf16[8,640,1024]{2,1,0:T(8,128)(2,1)} %get-tuple-element.87.refs_2_, ...), custom_call_target="tpu_custom_call" | custom-call | flops 80000000000 | bytes 250000000 | tf_op jit(solution)/shard_map/weight_grads/pallas_call | solution.py:215
  1188.4 10.9 maximum_select_fusion
  1199.4 58.1 %collective-permute-done.28 = bf16[8192,256]{1,0:T(8,128)(2,1)} collective-permute-done((bf16[8192,256]{1,0:T(8,128)(2,1)}, bf16[8192,256]{1,0:T(8,128)(2,1)}, u32[]{:S(2)}, u32[]{:S(2)}) %collective-permute-start.28) | collective-permute-done | bytes 4194336 | tf_op jit(solution)/shard_map/ppermute | solution.py:476
  1257.5 8.4 maximum_select_fusion.1
  (215 shorter events, 89.6 us)
Async XLA Ops:
  7.2 1178.5 %all-reduce.2.cloned.1.call-start = ((), (), s32[]{:S(2)}) async-start(), calls=%async_computation | async-start | bytes 163840 | tf_op jit(solution)/shard_map/psum | solution.py:605
  7.2 345.5 %collective-permute-start.2 = (bf16[8192,512]{1,0:T(8,128)(2,1)}, bf16[8192,512]{1,0:T(8,128)(2,1)}, u32[]{:S(2)}, u32[]{:S(2)}) collective-permute-start(bf16[8192,512]{1,0:T(8,128)(2,1)} %x_ref.3), channel_id=1, source_target_pairs={{0,1},{1,0},{2,3},{3,2},{4,5},{5,4},{6,7},{7,6}} | collective-permute-start | bytes 25165832 | tf_op jit(solution)/shard_map/ppermute | solution.py:473
  8.1 423.9 %collective-permute-start.7 = (bf16[8192,512]{1,0:T(8,128)(2,1)}, bf16[8192,512]{1,0:T(8,128)(2,1)}, u32[]{:S(2)}, u32[]{:S(2)}) collective-permute-start(bf16[8192,512]{1,0:T(8,128)(2,1)} %x_ref.3), channel_id=1, source_target_pairs={{0,2},{1,3},{2,0},{3,1},{4,6},{5,7},{6,4},{7,5}} | collective-permute-start | bytes 25165832 | tf_op jit(solution)/shard_map/ppermute | solution.py:473
  10.6 342.1 %collective-permute-start.3 = (bf16[8192,512]{1,0:T(8,128)(2,1)}, bf16[8192,512]{1,0:T(8,128)(2,1)}, u32[]{:S(2)}, u32[]{:S(2)}) collective-permute-start(bf16[8192,512]{1,0:T(8,128)(2,1)} %dy_ref.1), channel_id=1, source_target_pairs={{0,1},{1,0},{2,3},{3,2},{4,5},{5,4},{6,7},{7,6}} | collective-permute-start | bytes 25165832 | tf_op jit(solution)/shard_map/ppermute | solution.py:473
  15.5 335.3 %collective-permute-start.8 = (bf16[4096,512]{1,0:T(8,128)(2,1)}, bf16[4096,512]{1,0:T(8,128)(2,1)}, u32[]{:S(2)}, u32[]{:S(2)}) collective-permute-start(bf16[4096,512]{1,0:T(8,128)(2,1)} %constant_dynamic-slice_fusion), channel_id=1, source_target_pairs={{0,2},{1,3},{2,0},{3,1},{4,6},{5,7},{6,4},{7,5}} | collective-permute-start | bytes 12582920 | tf_op jit(solution)/shard_map/ppermute | solution.py:473
  23.5 267.4 %copy-start.4 = (s32[8192,1]{0,1:T(1,128)}, s32[8192,1]{0,1:T(1,128)S(1)}, u32[]{:S(2)}) copy-start(s32[8192,1]{0,1:T(1,128)S(1)} %get-tuple-element.128) | copy-start | bytes 98308
  23.5 275.6 %copy-start.7 = (s32[8192,1]{0,1:T(1,128)}, s32[8192,1]{0,1:T(1,128)S(1)}, u32[]{:S(2)}) copy-start(s32[8192,1]{0,1:T(1,128)S(1)} %get-tuple-element.127) | copy-start | bytes 98308
  304.2 33.8 %collective-permute-start.1 = (f32[2,8,640]{2,1,0:T(8,128)}, f32[2,8,640]{2,1,0:T(8,128)}, u32[]{:S(2)}, u32[]{:S(2)}) collective-permute-start(f32[2,8,640]{2,1,0:T(8,128)} %get-tuple-element.119), channel_id=1, source_target_pairs={{0,1},{1,0},{2,3},{3,2},{4,5},{5,4},{6,7},{7,6}} | collective-permute-start | bytes 122888 | tf_op jit(solution)/shard_map/ppermute | solution.py:473
  338.0 4.2 collective-permute-start.6
  342.2 5.8 collective-permute-start.12
  350.9 93.8 %collective-permute-start.9 = (bf16[4096,512]{1,0:T(8,128)(2,1)}, bf16[4096,512]{1,0:T(8,128)(2,1)}, u32[]{:S(2)}, u32[]{:S(2)}) collective-permute-start(bf16[4096,512]{1,0:T(8,128)(2,1)} %collective-permute-done.8.dya_ref), channel_id=1, source_target_pairs={{0,4},{4,0},{1,5},{5,1},{2,6},{6,2},{3,7},{7,3}} | collective-permute-start | bytes 12582920 | tf_op jit(solution)/shard_map/ppermute | solution.py:476
  352.4 173.3 %collective-permute-start.14 = (bf16[4096,512]{1,0:T(8,128)(2,1)}, bf16[4096,512]{1,0:T(8,128)(2,1)}, u32[]{:S(2)}, u32[]{:S(2)}) collective-permute-start(bf16[4096,512]{1,0:T(8,128)(2,1)} %collective-permute-done.8.dya_ref), channel_id=1, source_target_pairs={{0,1},{1,0},{2,3},{3,2},{4,5},{5,4},{6,7},{7,6}} | collective-permute-start | bytes 12582920 | tf_op jit(solution)/shard_map/ppermute | solution.py:473
  431.7 224.7 %collective-permute-start.4 = (bf16[8,640,256]{2,1,0:T(8,128)(2,1)}, bf16[8,640,256]{2,1,0:T(8,128)(2,1)}, u32[]{:S(2)}, u32[]{:S(2)}) collective-permute-start(bf16[8,640,256]{2,1,0:T(8,128)(2,1)} %get-tuple-element.62), channel_id=1, source_target_pairs={{0,4},{4,0},{1,5},{5,1},{2,6},{6,2},{3,7},{7,3}} | collective-permute-start | bytes 7864328 | tf_op jit(solution)/shard_map/ppermute | solution.py:476
  432.0 93.7 %collective-permute-start.13 = (bf16[8192,512]{1,0:T(8,128)(2,1)}, bf16[8192,512]{1,0:T(8,128)(2,1)}, u32[]{:S(2)}, u32[]{:S(2)}) collective-permute-start(bf16[8192,512]{1,0:T(8,128)(2,1)} %collective-permute-done.7.x_ref), channel_id=1, source_target_pairs={{0,1},{1,0},{2,3},{3,2},{4,5},{5,4},{6,7},{7,6}} | collective-permute-start | bytes 25165832 | tf_op jit(solution)/shard_map/ppermute | solution.py:473
  444.6 81.0 %collective-permute-start.15 = (bf16[4096,512]{1,0:T(8,128)(2,1)}, bf16[4096,512]{1,0:T(8,128)(2,1)}, u32[]{:S(2)}, u32[]{:S(2)}) collective-permute-start(bf16[4096,512]{1,0:T(8,128)(2,1)} %collective-permute-done.9.dyb_ref), channel_id=1, source_target_pairs={{0,1},{1,0},{2,3},{3,2},{4,5},{5,4},{6,7},{7,6}} | collective-permute-start | bytes 12582920 | tf_op jit(solution)/shard_map/ppermute | solution.py:473
  524.2 136.9 %collective-permute-start.10 = (bf16[8,640,256]{2,1,0:T(8,128)(2,1)}, bf16[8,640,256]{2,1,0:T(8,128)(2,1)}, u32[]{:S(2)}, u32[]{:S(2)}) collective-permute-start(bf16[8,640,256]{2,1,0:T(8,128)(2,1)} %get-tuple-element.66), channel_id=1, source_target_pairs={{0,4},{4,0},{1,5},{5,1},{2,6},{6,2},{3,7},{7,3}} | collective-permute-start | bytes 7864328 | tf_op jit(solution)/shard_map/ppermute | solution.py:476
  605.0 60.8 %collective-permute-start.16 = (bf16[8,640,256]{2,1,0:T(8,128)(2,1)}, bf16[8,640,256]{2,1,0:T(8,128)(2,1)}, u32[]{:S(2)}, u32[]{:S(2)}) collective-permute-start(bf16[8,640,256]{2,1,0:T(8,128)(2,1)} %get-tuple-element.70), channel_id=1, source_target_pairs={{0,4},{4,0},{1,5},{5,1},{2,6},{6,2},{3,7},{7,3}} | collective-permute-start | bytes 7864328 | tf_op jit(solution)/shard_map/ppermute | solution.py:476
  654.3 66.9 %collective-permute-start = (bf16[8,640,256]{2,1,0:T(8,128)(2,1)}, bf16[8,640,256]{2,1,0:T(8,128)(2,1)}, u32[]{:S(2)}, u32[]{:S(2)}) collective-permute-start(bf16[8,640,256]{2,1,0:T(8,128)(2,1)} %get-tuple-element.58), channel_id=1, source_target_pairs={{0,4},{4,0},{1,5},{5,1},{2,6},{6,2},{3,7},{7,3}} | collective-permute-start | bytes 7864328 | tf_op jit(solution)/shard_map/ppermute | solution.py:476
  655.9 121.6 %collective-permute-start.19 = (bf16[8,640,256]{2,1,0:T(8,128)(2,1)}, bf16[8,640,256]{2,1,0:T(8,128)(2,1)}, u32[]{:S(2)}, u32[]{:S(2)}) collective-permute-start(bf16[8,640,256]{2,1,0:T(8,128)(2,1)} %get-tuple-element.73), channel_id=1, source_target_pairs={{0,4},{4,0},{1,5},{5,1},{2,6},{6,2},{3,7},{7,3}} | collective-permute-start | bytes 7864328 | tf_op jit(solution)/shard_map/ppermute | solution.py:476
  656.4 177.2 %collective-permute-start.20 = (bf16[8,640,256]{2,1,0:T(8,128)(2,1)}, bf16[8,640,256]{2,1,0:T(8,128)(2,1)}, u32[]{:S(2)}, u32[]{:S(2)}) collective-permute-start(bf16[8,640,256]{2,1,0:T(8,128)(2,1)} %get-tuple-element.75), channel_id=1, source_target_pairs={{0,4},{4,0},{1,5},{5,1},{2,6},{6,2},{3,7},{7,3}} | collective-permute-start | bytes 7864328 | tf_op jit(solution)/shard_map/ppermute | solution.py:476
  661.1 228.0 %collective-permute-start.22 = (bf16[8,640,256]{2,1,0:T(8,128)(2,1)}, bf16[8,640,256]{2,1,0:T(8,128)(2,1)}, u32[]{:S(2)}, u32[]{:S(2)}) collective-permute-start(bf16[8,640,256]{2,1,0:T(8,128)(2,1)} %get-tuple-element.77), channel_id=1, source_target_pairs={{0,4},{4,0},{1,5},{5,1},{2,6},{6,2},{3,7},{7,3}} | collective-permute-start | bytes 7864328 | tf_op jit(solution)/shard_map/ppermute | solution.py:476
  665.8 228.0 %collective-permute-start.5 = (bf16[8,640,256]{2,1,0:T(8,128)(2,1)S(1)}, bf16[8,640,256]{2,1,0:T(8,128)(2,1)}, u32[]{:S(2)}, u32[]{:S(2)}) collective-permute-start(bf16[8,640,256]{2,1,0:T(8,128)(2,1)S(1)} %add_convert_fusion.6), channel_id=1, source_target_pairs={{0,1},{1,0},{2,3},{3,2},{4,5},{5,4},{6,7},{7,6}} | collective-permute-start | bytes 7864328 | tf_op jit(solution)/shard_map/ppermute | solution.py:473
  721.3 173.1 %collective-permute-start.11 = (bf16[8,640,256]{2,1,0:T(8,128)(2,1)}, bf16[8,640,256]{2,1,0:T(8,128)(2,1)}, u32[]{:S(2)}, u32[]{:S(2)}) collective-permute-start(bf16[8,640,256]{2,1,0:T(8,128)(2,1)} %add_convert_fusion.5), channel_id=1, source_target_pairs={{0,2},{1,3},{2,0},{3,1},{4,6},{5,7},{6,4},{7,5}} | collective-permute-start | bytes 7864328 | tf_op jit(solution)/shard_map/ppermute | solution.py:473
  777.4 116.9 %collective-permute-start.17 = (bf16[8,640,256]{2,1,0:T(8,128)(2,1)}, bf16[8,640,256]{2,1,0:T(8,128)(2,1)}, u32[]{:S(2)}, u32[]{:S(2)}) collective-permute-start(bf16[8,640,256]{2,1,0:T(8,128)(2,1)} %add_convert_fusion.4), channel_id=1, source_target_pairs={{0,3},{1,2},{2,1},{3,0},{4,7},{5,6},{6,5},{7,4}} | collective-permute-start | bytes 7864328 | tf_op jit(solution)/shard_map/ppermute | solution.py:473
  837.6 121.3 %collective-permute-start.21 = (bf16[8,640,256]{2,1,0:T(8,128)(2,1)}, bf16[8,640,256]{2,1,0:T(8,128)(2,1)}, u32[]{:S(2)}, u32[]{:S(2)}) collective-permute-start(bf16[8,640,256]{2,1,0:T(8,128)(2,1)} %add_convert_fusion.2), channel_id=1, source_target_pairs={{0,1},{1,0},{2,3},{3,2},{4,5},{5,4},{6,7},{7,6}} | collective-permute-start | bytes 7864328 | tf_op jit(solution)/shard_map/ppermute | solution.py:473
  893.0 65.9 %collective-permute-start.23 = (bf16[8,640,256]{2,1,0:T(8,128)(2,1)}, bf16[8,640,256]{2,1,0:T(8,128)(2,1)}, u32[]{:S(2)}, u32[]{:S(2)}) collective-permute-start(bf16[8,640,256]{2,1,0:T(8,128)(2,1)} %add_convert_fusion.1), channel_id=1, source_target_pairs={{0,2},{1,3},{2,0},{3,1},{4,6},{5,7},{6,4},{7,5}} | collective-permute-start | bytes 7864328 | tf_op jit(solution)/shard_map/ppermute | solution.py:473
  893.8 60.1 %collective-permute-start.24 = (bf16[8,640,256]{2,1,0:T(8,128)(2,1)}, bf16[8,640,256]{2,1,0:T(8,128)(2,1)}, u32[]{:S(2)}, u32[]{:S(2)}) collective-permute-start(bf16[8,640,256]{2,1,0:T(8,128)(2,1)} %get-tuple-element.79), channel_id=1, source_target_pairs={{0,4},{4,0},{1,5},{5,1},{2,6},{6,2},{3,7},{7,3}} | collective-permute-start | bytes 7864328 | tf_op jit(solution)/shard_map/ppermute | solution.py:476
  944.8 12.4 collective-permute-start.26
  957.2 59.0 %collective-permute-start.25 = (bf16[8,640,256]{2,1,0:T(8,128)(2,1)S(1)}, bf16[8,640,256]{2,1,0:T(8,128)(2,1)S(1)}, u32[]{:S(2)}, u32[]{:S(2)}) collective-permute-start(bf16[8,640,256]{2,1,0:T(8,128)(2,1)S(1)} %add_convert_fusion), channel_id=1, source_target_pairs={{0,3},{1,2},{2,1},{3,0},{4,7},{5,6},{6,5},{7,4}} | collective-permute-start | bytes 7864328 | tf_op jit(solution)/shard_map/ppermute | solution.py:473
  1068.1 9.5 collective-permute-start.27
  1071.7 116.7 %collective-permute-start.18 = (bf16[8192,256]{1,0:T(8,128)(2,1)}, bf16[8192,256]{1,0:T(8,128)(2,1)}, u32[]{:S(2)}, u32[]{:S(2)}) collective-permute-start(bf16[8192,256]{1,0:T(8,128)(2,1)} %get-tuple-element.71), channel_id=1, source_target_pairs={{0,4},{4,0},{1,5},{5,1},{2,6},{6,2},{3,7},{7,3}} | collective-permute-start | bytes 12582920 | tf_op jit(solution)/shard_map/ppermute | solution.py:476
  1093.7 163.8 %collective-permute-start.28 = (bf16[8192,256]{1,0:T(8,128)(2,1)}, bf16[8192,256]{1,0:T(8,128)(2,1)}, u32[]{:S(2)}, u32[]{:S(2)}) collective-permute-start(bf16[8192,256]{1,0:T(8,128)(2,1)} %finish_dx.1), channel_id=1, source_target_pairs={{0,4},{4,0},{1,5},{5,1},{2,6},{6,2},{3,7},{7,3}} | collective-permute-start | bytes 12582920 | tf_op jit(solution)/shard_map/ppermute | solution.py:476
  (42 other events, 2078.1 us)
Sparse Core Ops, SparseCore 0:
  1095.8 39.9 all-reduce.1

commit v2 on v1

--- a/solution.py
+++ b/solution.py
@@ -17,8 +17,16 @@
 VMEM_LIMIT = 64 * 1024 * 1024 - 128 * 1024
 
 
-def row_gather_kernel(split, blocks, tok_ref, side_ref, x_ref, dya_ref, dyb_ref, scale_ref, gate_ref,
-                      u_ref, do_ref, table, rows_buf):
+def part_slot(p, part_count, side):
+    if part_count == 1:
+        return 0
+    per_half = part_count // 2
+    own = p < per_half
+    return (side if own else 1 - side) * per_half + p % per_half
+
+
+def row_gather_kernel(part_count, blocks, tok_ref, side_ref, x_ref, *refs):
+    dy_refs, (scale_ref, gate_ref, u_ref, do_ref, table, rows_buf) = refs[:part_count], refs[part_count:]
     step = pl.program_id(0)
     tok_block, width = x_ref.shape
     slices = width // LANES
@@ -30,11 +38,10 @@
         x_wide = x_ref[...].astype(jnp.float32)
         inv_rms = lax.rsqrt(jnp.mean(x_wide * x_wide, axis=-1, keepdims=True) + NORM_EPS)
         u_wide = (x_wide * inv_rms * scale_ref[...]).astype(jnp.bfloat16).astype(jnp.float32)
-        if split:
-            half = blocks // 2
-            dy_val = jnp.where(step // half == side_ref[0], dya_ref[...], dyb_ref[...]).astype(jnp.float32)
-        else:
-            dy_val = dya_ref[...].astype(jnp.float32)
+        dy_val = dy_refs[0][...]
+        for p in range(1, part_count):
+            dy_val = jnp.where(step // (blocks // part_count) == part_slot(p, part_count, side_ref[0]), dy_refs[p][...], dy_val)
+        dy_val = dy_val.astype(jnp.float32)
         base = pl.multiple_of(step * (tok_block * tile), tile)
         for k in range(slices):
             cols = slice(k * LANES, (k + 1) * LANES)
@@ -72,29 +79,22 @@
     local_exp, slot_cap, _ = gate_col.shape
     tok_block = 512
     blocks = tok_count // tok_block
-    half = blocks // 2
     tile = 2 * width // LANES
-    split = len(dy_parts) == 2
-    if split:
-        dya, dyb = dy_parts
-        map_a = lambda i, tok, sd: (jnp.clip(i - sd[0] * half, 0, half - 1), 0)
-        map_b = lambda i, tok, sd: (jnp.clip(i - (1 - sd[0]) * half, 0, half - 1), 0)
-    else:
-        dya = dyb = dy_parts[0]
-        map_a = lambda i, tok, sd: (jnp.minimum(i, blocks - 1), 0)
-        map_b = lambda i, tok, sd: (0, 0)
+    part_count = len(dy_parts)
+    each = blocks // part_count
+    part_maps = [(lambda p: lambda i, tok, sd: (jnp.clip(i - part_slot(p, part_count, sd[0]) * each, 0, each - 1), 0))(p)
+                 for p in range(part_count)]
     exp_map = lambda i, tok, sd: (jnp.maximum(i - blocks, 0), 0, 0)
     tok_spec = (tok_block, width)
     row_shape = jax.ShapeDtypeStruct((local_exp, slot_cap, width), jnp.bfloat16)
     return pl.pallas_call(
-        functools.partial(row_gather_kernel, split, blocks),
+        functools.partial(row_gather_kernel, part_count, blocks),
         grid_spec=pltpu.PrefetchScalarGridSpec(
             num_scalar_prefetch=2,
             grid=(blocks + local_exp,),
             in_specs=[
                 pl.BlockSpec(tok_spec, lambda i, tok, sd: (jnp.minimum(i, blocks - 1), 0)),
-                pl.BlockSpec(tok_spec, map_a),
-                pl.BlockSpec(tok_spec, map_b),
+                *[pl.BlockSpec(tok_spec, m) for m in part_maps],
                 pl.BlockSpec((1, width), lambda i, tok, sd: (0, 0)),
                 pl.BlockSpec((1, slot_cap, 1), exp_map),
             ],
@@ -108,7 +108,7 @@
         compiler_params=pltpu.CompilerParams(vmem_limit_bytes=VMEM_LIMIT, dimension_semantics=("arbitrary",)),
         cost_estimate=pl.CostEstimate(flops=30_000_000_000, bytes_accessed=40_000_000, transcendentals=0),
         name="gather_rows",
-    )(slot_tok, side, x_grp, dya, dyb, scale_row, gate_col)
+    )(slot_tok, side, x_grp, *dy_parts, scale_row, gate_col)
 
 
 def dot_nt(lhs, rhs):
@@ -187,44 +187,44 @@
     )(side, u_rows, do_rows, gate_loc, lin_loc, out_loc)
 
 
-def weight_grad_kernel(groups, *refs):
-    ins, (dg_ref, dl_ref, dw_ref) = refs[:5 * groups], refs[5 * groups:]
-    d_gate = d_lin = d_out = None
+def weight_grad_kernel(groups, carried, *refs):
+    ins = refs[:5 * groups]
+    sums = refs[5 * groups:5 * groups + carried]
+    outs = refs[5 * groups + carried:]
+    acc = [ref[0] for ref in sums] if carried else [None] * 3
     for g in range(groups):
         u_ref, do_ref, h_ref, da0_ref, da1_ref = ins[5 * g:5 * g + 5]
-        pg = dot_tn(u_ref[0], da0_ref[0])
-        pn = dot_tn(u_ref[0], da1_ref[0])
-        po = dot_tn(h_ref[0], do_ref[0])
-        d_gate = pg if d_gate is None else d_gate + pg
-        d_lin = pn if d_lin is None else d_lin + pn
-        d_out = po if d_out is None else d_out + po
-    dg_ref[0] = d_gate
-    dl_ref[0] = d_lin
-    dw_ref[0] = d_out
-
-
-def weight_grads(parts):
+        terms = (dot_tn(u_ref[0], da0_ref[0]), dot_tn(u_ref[0], da1_ref[0]), dot_tn(h_ref[0], do_ref[0]))
+        acc = [t if a is None else a + t for a, t in zip(acc, terms)]
+    for ref, val in zip(outs, acc):
+        ref[0] = val
+
+
+def weight_grads(parts, carry=()):
     local_exp, slot_cap, width = parts[0][0].shape
     ff = parts[0][2].shape[2]
-    splits = 2
+    splits = 1
     ff_blk = ff // splits
     row_block = pl.BlockSpec((1, slot_cap, width), lambda e, f: (e, 0, 0))
     ff_block = pl.BlockSpec((1, slot_cap, ff_blk), lambda e, f: (e, 0, f))
     in_shape = jax.ShapeDtypeStruct((local_exp, width, ff), jnp.float32)
     out_shape = jax.ShapeDtypeStruct((local_exp, ff, width), jnp.float32)
+    grad_specs = [pl.BlockSpec((1, width, ff_blk), lambda e, f: (e, 0, f)),
+                  pl.BlockSpec((1, width, ff_blk), lambda e, f: (e, 0, f)),
+                  pl.BlockSpec((1, ff_blk, width), lambda e, f: (e, f, 0))]
+    first = 5 * len(parts)
     return pl.pallas_call(
-        functools.partial(weight_grad_kernel, len(parts)),
+        functools.partial(weight_grad_kernel, len(parts), len(carry)),
         grid=(local_exp, splits),
-        in_specs=[row_block, row_block, ff_block, ff_block, ff_block] * len(parts),
-        out_specs=[pl.BlockSpec((1, width, ff_blk), lambda e, f: (e, 0, f)),
-                   pl.BlockSpec((1, width, ff_blk), lambda e, f: (e, 0, f)),
-                   pl.BlockSpec((1, ff_blk, width), lambda e, f: (e, f, 0))],
+        in_specs=[row_block, row_block, ff_block, ff_block, ff_block] * len(parts) + (grad_specs if carry else []),
+        out_specs=grad_specs,
         out_shape=[in_shape, in_shape, out_shape],
+        input_output_aliases={first + i: i for i in range(len(carry))},
         compiler_params=pltpu.CompilerParams(vmem_limit_bytes=VMEM_LIMIT,
                                              dimension_semantics=("arbitrary", "arbitrary")),
-        cost_estimate=pl.CostEstimate(flops=80_000_000_000, bytes_accessed=250_000_000, transcendentals=0),
+        cost_estimate=pl.CostEstimate(flops=50_000_000_000, bytes_accessed=150_000_000, transcendentals=0),
         name="weight_grads",
-    )(*[a for part in parts for a in part])
+    )(*[a for part in parts for a in part], *carry)
 
 
 def rows_to_cols(rows):
@@ -455,10 +455,25 @@
     )(side, du_all, x_loc, dy_loc, feat, part_a, part_b, scale_half)
 
 
-def slot_positions(hit_first, hit_second):
-    rank_first = jnp.cumsum(hit_first, axis=0) - hit_first
-    rank_second = jnp.cumsum(hit_second, axis=0) - hit_second + jnp.sum(hit_first, axis=0)
-    return jnp.sum(rank_first * hit_first, axis=1), jnp.sum(rank_second * hit_second, axis=1)
+def strict_lower(size):
+    idx = jnp.arange(size, dtype=jnp.int32)
+    return (idx[None, :] < idx[:, None]).astype(jnp.bfloat16)
+
+
+def slot_positions(one_first, one_second):
+    tok_count, experts = one_first.shape
+    blk = 128
+    hits = jnp.concatenate([one_first, one_second], axis=1)
+    blocks = hits.astype(jnp.bfloat16).reshape(tok_count // blk, blk, 2 * experts)
+    inner = jnp.einsum('ij,bje->bie', strict_lower(blk), blocks, preferred_element_type=jnp.float32)
+    totals = jnp.sum(blocks.astype(jnp.float32), axis=1)
+    outer = jnp.dot(strict_lower(tok_count // blk), totals.astype(jnp.bfloat16), preferred_element_type=jnp.float32)
+    first_total = jnp.sum(totals[:, :experts], axis=0)
+    shift = jnp.concatenate([jnp.zeros_like(first_total), first_total])
+    rank = (inner + (outer + shift)[:, None, :]).reshape(tok_count, 2 * experts) * hits
+    pos_first = jnp.sum(rank[:, :experts], axis=1).astype(jnp.int32)
+    pos_second = jnp.sum(rank[:, experts:], axis=1).astype(jnp.int32)
+    return pos_first, pos_second, first_total
 
 
 def round_bf16(val):
@@ -486,17 +501,20 @@
         side = lax.axis_index('tp')
         side_arr = side.astype(jnp.int32).reshape(1)
 
+        quarter = tok_count // 4
         dy_half = lax.dynamic_slice_in_dim(dy_loc, side * (tok_count // 2), tok_count // 2, axis=0)
-        dy2_a = swap_ep(dy_half, 2)
+        dy2_p = swap_ep(dy_half[:quarter], 2)
+        dy2_q = swap_ep(dy_half[quarter:], 2)
         x2 = swap_ep(x_loc, 2)
-        dy2_b = swap_tp(dy2_a)
+        dy2_r = swap_tp(dy2_p)
+        dy2_s = swap_tp(dy2_q)
         x1 = swap_ep(x_loc, 1)
         dy1 = swap_ep(dy_loc, 1)
         x3 = swap_ep(x2, 1)
-        dy3_a = swap_ep(dy2_a, 1)
-        dy3_b = swap_ep(dy2_b, 1)
+        dy2 = (dy2_p, dy2_q, dy2_r, dy2_s)
+        dy3 = tuple(swap_ep(d, 1) for d in dy2)
         x_grp = (x_loc, x1, x2, x3)
-        dy_grp = ((dy_loc,), (dy1,), (dy2_a, dy2_b), (dy3_a, dy3_b))
+        dy_grp = ((dy_loc,), (dy1,), dy2, dy3)
 
         x_wide = x_loc.astype(jnp.float32)
         inv_rms = lax.rsqrt(jnp.mean(x_wide * x_wide, axis=-1, keepdims=True) + NORM_EPS)
@@ -516,7 +534,7 @@
         norm_first = gate_first / gate_total
         norm_second = gate_second / gate_total
 
-        pos_first, pos_second = slot_positions(hit_first.astype(jnp.int32), hit_second.astype(jnp.int32))
+        pos_first, pos_second, first_total = slot_positions(one_first, one_second)
         tok_ids = jnp.arange(tok_count, dtype=jnp.int32)
         tok_hi = (tok_ids // 64).astype(jnp.float32)
         tok_lo = (tok_ids % 64).astype(jnp.float32)
@@ -534,16 +552,27 @@
         slot_tok = jnp.where(table[0] > 0.5, table[1] * 64.0 + table[2], float(tok_count))
         slot_gate = table[3] + table[4] + table[5]
         slot_pack = jnp.stack([slot_tok, slot_gate]).reshape(2, ep_size, local_exp, slot_cap)
+        stats = jnp.concatenate([first_total, jnp.sum(router_prob, axis=0), jnp.sum(log_norm * log_norm).reshape(1)])
+        stats_row = jnp.pad(stats, (0, local_exp * slot_cap - stats.shape[0])).reshape(1, local_exp, slot_cap)
+        grp_stats = []
 
         scale_row = norm_scale.reshape(1, width)
+        near = ep_size // 2
         saved = {}
         back_o = [None] * ep_size
         back_du = [None] * ep_size
         sent = {}
         for bit in range(ep_size):
             pack = lax.dynamic_index_in_dim(slot_pack, me ^ bit, axis=1, keepdims=False)
+            pack = jnp.concatenate([pack, stats_row])
             if bit:
                 pack = swap_ep(pack, bit)
+            if bit == near:
+                grads = weight_grads([saved[b] for b in range(near)])
+                after_near = grads[2][0, 0, :8]
+            if bit >= near:
+                pack, _ = lax.optimization_barrier((pack, after_near))
+            grp_stats.append(pack[2].reshape(local_exp * slot_cap)[:stats.shape[0]])
             tok_grp = pack[0].astype(jnp.int32).reshape(local_exp * slot_cap)
             gate_grp = pack[1].reshape(local_exp, slot_cap, 1)
             u_rows, do_rows = gather_rows(tok_grp, side_arr, x_grp[bit], dy_grp[bit], scale_row, gate_grp)
@@ -562,7 +591,7 @@
                 du_sum = swap_ep(du_sum, bit)
             back_o[bit] = o_sum
             back_du[bit] = du_sum
-        d_gate, d_lin, d_out = weight_grads([saved[b] for b in range(ep_size)])
+        d_gate, d_lin, d_out = weight_grads([saved[b] for b in range(near, ep_size)], grads)
 
         per_dev = local_exp * slot_cap
 
@@ -580,9 +609,7 @@
         part_o = part_o + swap_tp(part_o)
         dn_first, dn_second = part_o[0], part_o[1]
 
-        stats = jnp.concatenate([jnp.sum(one_first, axis=0), jnp.sum(router_prob, axis=0),
-                                 jnp.sum(log_norm * log_norm).reshape(1)])
-        stats = lax.psum(stats, 'ep')
+        stats = (grp_stats[0] + grp_stats[1]) + (grp_stats[2] + grp_stats[3])
         first_count, prob_sum, norm_sq = stats[:experts], stats[experts:2 * experts], stats[2 * experts]
         frac_first = first_count / tokens
         z_loss = Z_COEF * norm_sq / tokens
@@ -598,11 +625,12 @@
             rows, side_arr, back_du, x_loc, feat, d_logits.T, half_of(w_router, 0).T, scale_half)
         part_other = swap_tp(part_du)
         dx_half = finish_dx(side_arr, du_all, x_loc, dy_loc, feat, part_du, part_other, scale_half)
+        dx_other = swap_tp(dx_half)
         sums = jnp.concatenate([d_router_half, d_scale_half])
-        dx_half, sums = lax.optimization_barrier((dx_half, sums))
-        dx_other = swap_tp(dx_half)
-        sums = lax.dynamic_update_slice_in_dim(jnp.zeros((experts + 1, width), jnp.float32), sums, side * half, axis=1)
-        sums = lax.psum(sums, ('ep', 'tp'))
+        sums = sums + swap_ep(sums, 1)
+        sums = sums + swap_ep(sums, 2)
+        sums_other = swap_tp(sums)
+        sums = jnp.where(side == 0, jnp.concatenate([sums, sums_other], axis=1), jnp.concatenate([sums_other, sums], axis=1))
         d_router = sums[:experts].T
         d_scale = sums[experts]
 

time: 1280 us -> 1190 us (0.930)
  blocking collectives: 235 us -> 0 us
  waiting for transfers between devices: 343 us -> 474 us
  Pallas kernels: 524 us -> 547 us
  other arithmetic: 92.6 us -> 76.3 us
  between operations: 16.5 us -> 2.99 us
    psum x1 -> x0, blocking collectives: 235 us -> none  [device_body(): stats = lax.psum(stats, 'ep')]
    ppermute x13 -> x15, waiting for transfers between devices: 283 us -> 362 us  [swap_tp(): return lax.ppermute(val, 'tp', [(i, i ^ 1) for i in range(tp_size)])]
    ppermute x16 -> x21, waiting for transfers between devices: 60.5 us -> 112 us  [swap_ep(): return lax.ppermute(val, 'ep', [(i, i ^ bit) for i in range(ep_size)])]
    pallas_call x5 -> x6, Pallas kernels: 213 us -> 235 us  [the longest x4 124 us: gather_rows(): pl.pallas_call(functools.partial(row_gather_kernel, part_count, blocks),...]
    another operation x6 -> x0, other arithmetic: 20.2 us -> none
  transfers between devices with their start and end apart: 30 -> 36, of which waited for: 10 -> 14; matrix products, arithmetic and copies ran while one was open for 10% -> 9% of each run, Pallas kernels for 37% -> 42%
where the time goes in v2:
time: 1190 us; the launch traced here: 1180 us
  Pallas kernels  547 us (46%)
  waiting for transfers between devices  474 us (40%)
  other arithmetic  76.3 us (6%)
  starting transfers between devices  31.7 us (3%)
  local copies, waits for them, and re-layouts  30.3 us (3%)
  matrix products  16.3 us (1%)
    ppermute x15, waiting for transfers between devices, swap_tp(): return lax.ppermute(val, 'tp', [(i, i ^ 1) for i in range(tp_size)])  362 us
    pallas_call x4, Pallas kernels, run_experts(): pl.pallas_call(expert_kernel, grid_spec=pltpu.PrefetchScalarGridSpec(num_...  195 us
    pallas_call x4, Pallas kernels, gather_rows(): pl.pallas_call(functools.partial(row_gather_kernel, part_count, blocks),...  124 us
    ppermute x21, waiting for transfers between devices, swap_ep(): return lax.ppermute(val, 'ep', [(i, i ^ bit) for i in range(ep_size)])  112 us
    pallas_call x2, Pallas kernels, weight_grads(): pl.pallas_call(functools.partial(weight_grad_kernel, len(parts), len(carr...  110 us
    pallas_call x2, Pallas kernels, combine_call(): pl.pallas_call(functools.partial(kernel, table_steps, groups), grid_spec=...  101 us
  transfers between devices with their start and end apart: 36, of which 14 were waited for; matrix products, arithmetic and copies ran while one was open for 9% of the time, Pallas kernels for 42%

profile of v2, /device:TPU:0, one launch (start us, length us, event | category | flops | bytes accessed | tf_op | source)
XLA Modules:
  0.0 1178.7 jit_solution(5970944427872698789)
XLA Ops:
  3.9 5.1 fusion.2
  9.1 6.7 fusion.76
  23.4 4.2 fusion
  27.9 4.7 fusion.11
  34.6 4.5 constant_dynamic-slice_fusion
  44.5 30.0 %gather_rows.4 = (bf16[8,640,512]{2,1,0:T(8,128)(2,1)}, bf16[8,640,512]{2,1,0:T(8,128)(2,1)}) custom-call(s32[5120]{0:T(1024)} %convert_element_type.177.tok_ref, s32[1]{0:T(128)} %bitcast.6.side_ref, bf16[8192,512]{1,0:T(8,128)(2,1)} %x_ref.3, bf16[8192,512]{1,0:T(8,128)(2,1)} %dy_ref.1, f32[1,512]{1,0:T(1,128)} %bitcast.88, f32[8,640,1]{2,1,0:T(8,128)} %copy.32.refs_2_), custom_call_target="tpu_custom_call" | custom-call | flops 30000001024 | bytes 40000000 | tf_op jit(solution)/shard_map/gather_rows/pallas_call | solution.py:90
  74.5 48.6 %expert_pass.4 = (bf16[8,640,256]{2,1,0:T(8,128)(2,1)}, bf16[8,640,256]{2,1,0:T(8,128)(2,1)}, bf16[8,640,256]{2,1,0:T(8,128)(2,1)}, bf16[8,640,256]{2,1,0:T(8,12...) custom-call(s32[1]{0:T(128)} %bitcast.6.side_ref, ...), custom_call_target="tpu_custom_call" | custom-call | flops 60000002048 | bytes 100000000 | tf_op jit(solution)/shard_map/expert_pass/pallas_call | solution.py:175
  136.1 30.0 %gather_rows.5 = (bf16[8,640,512]{2,1,0:T(8,128)(2,1)}, bf16[8,640,512]{2,1,0:T(8,128)(2,1)}) custom-call(s32[5120]{0:T(1024)} %convert_element_type.182.tok_ref, s32[1]{0:T(128)} %bitcast.6.side_ref, bf16[8192,512]{1,0:T(8,128)(2,1)} %collective-permute-done.2.x_ref, bf16[8192,512]{1,0:T(8,128)(2,1)} %collective-permute-done.3.refs_0_, f32[1,512]{1,0:T(1,128)} %bitcast.89, ...), custom_call_target="tpu_custom_call" | custom-call | flops 30000001024 | bytes 40000000 | tf_op jit(solution)/shard_map/gather_rows/pallas_call | solution.py:90
  166.2 48.8 %expert_pass.5 = (bf16[8,640,256]{2,1,0:T(8,128)(2,1)}, bf16[8,640,256]{2,1,0:T(8,128)(2,1)}, bf16[8,640,256]{2,1,0:T(8,128)(2,1)}, bf16[8,640,256]{2,1,0:T(8,12...) custom-call(s32[1]{0:T(128)} %bitcast.6.side_ref, ...), custom_call_target="tpu_custom_call" | custom-call | flops 60000002048 | bytes 100000000 | tf_op jit(solution)/shard_map/expert_pass/pallas_call | solution.py:175
  215.0 47.8 %weight_grads.2 = (f32[8,512,1024]{2,1,0:T(8,128)}, f32[8,512,1024]{2,1,0:T(8,128)}, f32[8,1024,512]{2,1,0:T(8,128)}) custom-call(bf16[8,640,512]{2,1,0:T(8,128)(2,1)} %get-tuple-element.58.u_ref.refs_0_, bf16[8,640,512]{2,1,0:T(8,128)(2,1)} %get-tuple-element.59.do_ref.refs_1_, bf16[8,640,1024]{2,1,0:T(8,128)(2,1)} %get-tuple-element.66.refs_2_, ...), custom_call_target="tpu_custom_call" | custom-call | flops 49999998976 | bytes 150000000 | tf_op jit(solution)/shard_map/weight_grads/pallas_call | solution.py:216
  262.8 51.6 %collective-permute-done.6 = f32[3,8,640]{2,1,0:T(8,128)} collective-permute-done((f32[3,8,640]{2,1,0:T(8,128)}, f32[3,8,640]{2,1,0:T(8,128)}, u32[]{:S(2)}, u32[]{:S(2)}) %collective-permute-start.6) | collective-permute-done | bytes 61472 | tf_op jit(solution)/shard_map/ppermute | solution.py:488
  319.7 32.1 %gather_rows.6 = (bf16[8,640,512]{2,1,0:T(8,128)(2,1)}, bf16[8,640,512]{2,1,0:T(8,128)(2,1)}) custom-call(s32[5120]{0:T(1024)} %convert_element_type.187.tok_ref, s32[1]{0:T(128)} %bitcast.6.side_ref, bf16[8192,512]{1,0:T(8,128)(2,1)} %collective-permute-done.7.x_ref, bf16[2048,512]{1,0:T(8,128)(2,1)} %collective-permute-done.8.refs_0_, ...), custom_call_target="tpu_custom_call" | custom-call | flops 30000001024 | bytes 40000000 | tf_op jit(solution)/shard_map/gather_rows/pallas_call | solution.py:90
  351.8 48.8 %expert_pass.6 = (bf16[8,640,256]{2,1,0:T(8,128)(2,1)}, bf16[8,640,256]{2,1,0:T(8,128)(2,1)}, bf16[8,640,256]{2,1,0:T(8,128)(2,1)}, bf16[8,640,256]{2,1,0:T(8,12...) custom-call(s32[1]{0:T(128)} %bitcast.6.side_ref, ...), custom_call_target="tpu_custom_call" | custom-call | flops 60000002048 | bytes 100000000 | tf_op jit(solution)/shard_map/expert_pass/pallas_call | solution.py:175
  409.0 32.2 %gather_rows.7 = (bf16[8,640,512]{2,1,0:T(8,128)(2,1)}, bf16[8,640,512]{2,1,0:T(8,128)(2,1)}) custom-call(s32[5120]{0:T(1024)} %convert_element_type.192.tok_ref, s32[1]{0:T(128)} %bitcast.6.side_ref, bf16[8192,512]{1,0:T(8,128)(2,1)} %collective-permute-done.15.x_ref, bf16[2048,512]{1,0:T(8,128)(2,1)} %collective-permute-done.16.refs_0_, ...), custom_call_target="tpu_custom_call" | custom-call | flops 30000001024 | bytes 40000000 | tf_op jit(solution)/shard_map/gather_rows/pallas_call | solution.py:90
  441.2 49.0 %expert_pass.7 = (bf16[8,640,256]{2,1,0:T(8,128)(2,1)}, bf16[8,640,256]{2,1,0:T(8,128)(2,1)}, bf16[8,640,256]{2,1,0:T(8,128)(2,1)}, bf16[8,640,256]{2,1,0:T(8,12...) custom-call(s32[1]{0:T(128)} %bitcast.6.side_ref, ...), custom_call_target="tpu_custom_call" | custom-call | flops 60000002048 | bytes 100000000 | tf_op jit(solution)/shard_map/expert_pass/pallas_call | solution.py:175
  494.7 82.6 %collective-permute-done.4 = bf16[8,640,256]{2,1,0:T(8,128)(2,1)} collective-permute-done((bf16[8,640,256]{2,1,0:T(8,128)(2,1)}, bf16[8,640,256]{2,1,0:T(8,128)(2,1)}, u32[]{:S(2)}, u32[]{:S(2)}) %collective-permute-start.4) | collective-permute-done | bytes 2621472 | tf_op jit(solution)/shard_map/ppermute | solution.py:491
  579.4 4.8 add_convert_fusion.6
  584.1 49.4 %collective-permute-done.12 = bf16[8,640,256]{2,1,0:T(8,128)(2,1)} collective-permute-done((bf16[8,640,256]{2,1,0:T(8,128)(2,1)}, bf16[8,640,256]{2,1,0:T(8,128)(2,1)}, u32[]{:S(2)}, u32[]{:S(2)}) %collective-permute-start.12) | collective-permute-done | bytes 2621472 | tf_op jit(solution)/shard_map/ppermute | solution.py:491
  639.6 49.9 %collective-permute-done.20 = bf16[8,640,256]{2,1,0:T(8,128)(2,1)S(1)} collective-permute-done((bf16[8,640,256]{2,1,0:T(8,128)(2,1)}, bf16[8,640,256]{2,1,0:T(8,128)(2,1)S(1)}, u32[]{:S(2)}, u32[]{:S(2)}) %collective-permute-start.20) | collective-permute-done | bytes 2621472 | tf_op jit(solution)/shard_map/ppermute | solution.py:491
  709.0 36.9 %collective-permute-done.24 = bf16[8,640,256]{2,1,0:T(8,128)(2,1)} collective-permute-done((bf16[8,640,256]{2,1,0:T(8,128)(2,1)}, bf16[8,640,256]{2,1,0:T(8,128)(2,1)}, u32[]{:S(2)}, u32[]{:S(2)}) %collective-permute-start.24) | collective-permute-done | bytes 2621472 | tf_op jit(solution)/shard_map/ppermute | solution.py:491
  745.9 4.9 add_convert_fusion.2
  750.7 51.1 %collective-permute-done.26 = bf16[8,640,256]{2,1,0:T(8,128)(2,1)} collective-permute-done((bf16[8,640,256]{2,1,0:T(8,128)(2,1)}, bf16[8,640,256]{2,1,0:T(8,128)(2,1)}, u32[]{:S(2)}, u32[]{:S(2)}) %collective-permute-start.26) | collective-permute-done | bytes 2621472 | tf_op jit(solution)/shard_map/ppermute | solution.py:491
  810.7 50.4 %shard_map.143 = (bf16[8192,256]{1,0:T(8,128)(2,1)}, f32[8,8192]{1,0:T(8,128)}) custom-call(s32[8192]{0:T(1024)} %get-tuple-element.163.row1_ref, s32[8192]{0:T(1024)} %get-tuple-element.164.row2_ref, s32[1]{0:T(128)} %bitcast.6.side_ref, bf16[8,640,256]{2,1,0:T(8,128)(2,1)} %add_convert_fusion.7.refs_0_, ...), custom_call_target="tpu_custom_call" | custom-call | flops 49999998976 | bytes 40000000 | tf_op jit(solution)/shard_map/pallas_call | solution.py:378
  862.7 4.2 collective-permute-done.28
  873.1 54.4 %collective-permute-done.29.refs_3_ = bf16[8,640,256]{2,1,0:T(8,128)(2,1)S(1)} collective-permute-done((bf16[8,640,256]{2,1,0:T(8,128)(2,1)S(1)}, bf16[8,640,256]{2,1,0:T(8,128)(2,1)S(1)}, u32[]{:S(2)}, u32[]{:S(2)}) %collective-permute-start.29) | collective-permute-done | bytes 2621472 | tf_op jit(solution)/shard_map/ppermute | solution.py:488
  929.1 50.4 %shard_map.144 = (f32[8192,256]{1,0:T(8,128)}, f32[8,8192]{1,0:T(8,128)}, f32[32,256]{1,0:T(8,128)}, f32[1,256]{1,0:T(1,128)}) custom-call(s32[8192]{0:T(1024)} %get-tuple-element.163.row1_ref, s32[8192]{0:T(1024)} %get-tuple-element.164.row2_ref, s32[1]{0:T(128)} %bitcast.6.side_ref, bf16[8,640,256]{2,1,0:T(8,128)(2,1)} %add_convert_fusion.3.refs_0_, ...), custom_call_target="tpu_custom_call" | custom-call | flops 49999998976 | bytes 40000000 | tf_op jit(solution)/shard_map/pallas_call | solution.py:378
  990.4 16.2 %finish_dx.1 = bf16[8192,256]{1,0:T(8,128)(2,1)} custom-call(s32[1]{0:T(128)} %bitcast.6.side_ref, f32[8192,256]{1,0:T(8,128)} %get-tuple-element.93.du_ref, bf16[8192,512]{1,0:T(8,128)(2,1)} %x_ref.3, bf16[8192,512]{1,0:T(8,128)(2,1)} %dy_ref.1, f32[8,8192]{1,0:T(8,128)} %stack.22.refs_6_.refs_5_.feat_ref, f32[8,8192]{1,0:T(8,128)} %get-tuple-element.94.part_a_ref, ...), custom_call_target="tpu_custom_call" | custom-call | flops 10000000000 | bytes 20000000 | tf_op jit(solution)/shard_map/finish_dx/pallas_call | solution.py:441
  1008.0 62.6 %weight_grads.3 = (f32[8,512,1024]{2,1,0:T(8,128)}, f32[8,512,1024]{2,1,0:T(8,128)}, f32[8,1024,512]{2,1,0:T(8,128)}) custom-call(bf16[8,640,512]{2,1,0:T(8,128)(2,1)} %get-tuple-element.74.u_ref.refs_0_, bf16[8,640,512]{2,1,0:T(8,128)(2,1)} %get-tuple-element.75.do_ref.refs_1_, ...), custom_call_target="tpu_custom_call", output_to_operand_aliasing={{0}: (10, {}), {1}: (11, {}), {2}: (12, {})} | custom-call | flops 49999998976 | bytes 150000000 | tf_op jit(solution)/shard_map/weight_grads/pallas_call | solution.py:216
  1070.6 10.7 collective-permute-done.35
  1083.5 10.9 maximum_select_fusion
  1094.4 75.8 %collective-permute-done.32 = bf16[8192,256]{1,0:T(8,128)(2,1)} collective-permute-done((bf16[8192,256]{1,0:T(8,128)(2,1)}, bf16[8192,256]{1,0:T(8,128)(2,1)}, u32[]{:S(2)}, u32[]{:S(2)}) %collective-permute-start.32) | collective-permute-done | bytes 4194336 | tf_op jit(solution)/shard_map/ppermute | solution.py:491
  1170.2 8.3 maximum_select_fusion.1
  (241 shorter events, 107.9 us)
Async XLA Ops:
  0.6 133.5 %collective-permute-start.2 = (bf16[8192,512]{1,0:T(8,128)(2,1)}, bf16[8192,512]{1,0:T(8,128)(2,1)}, u32[]{:S(2)}, u32[]{:S(2)}) collective-permute-start(bf16[8192,512]{1,0:T(8,128)(2,1)} %x_ref.3), channel_id=1, source_target_pairs={{0,1},{1,0},{2,3},{3,2},{4,5},{5,4},{6,7},{7,6}} | collective-permute-start | bytes 25165832 | tf_op jit(solution)/shard_map/ppermute | solution.py:488
  34.1 90.4 %collective-permute-start.1 = (f32[3,8,640]{2,1,0:T(8,128)}, f32[3,8,640]{2,1,0:T(8,128)}, u32[]{:S(2)}, u32[]{:S(2)}) collective-permute-start(f32[3,8,640]{2,1,0:T(8,128)} %get-tuple-element.154), channel_id=1, source_target_pairs={{0,1},{1,0},{2,3},{3,2},{4,5},{5,4},{6,7},{7,6}} | collective-permute-start | bytes 184328 | tf_op jit(solution)/shard_map/ppermute | solution.py:488
  34.1 101.5 %collective-permute-start.3 = (bf16[8192,512]{1,0:T(8,128)(2,1)}, bf16[8192,512]{1,0:T(8,128)(2,1)}, u32[]{:S(2)}, u32[]{:S(2)}) collective-permute-start(bf16[8192,512]{1,0:T(8,128)(2,1)} %dy_ref.1), channel_id=1, source_target_pairs={{0,1},{1,0},{2,3},{3,2},{4,5},{5,4},{6,7},{7,6}} | collective-permute-start | bytes 25165832 | tf_op jit(solution)/shard_map/ppermute | solution.py:488
  39.1 91.6 %collective-permute-start.8 = (bf16[2048,512]{1,0:T(8,128)(2,1)}, bf16[2048,512]{1,0:T(8,128)(2,1)}, u32[]{:S(2)}, u32[]{:S(2)}) collective-permute-start(bf16[2048,512]{1,0:T(8,128)(2,1)} %get-tuple-element.120), channel_id=1, source_target_pairs={{0,2},{1,3},{2,0},{3,1},{4,6},{5,7},{6,4},{7,5}} | collective-permute-start | bytes 6291464 | tf_op jit(solution)/shard_map/ppermute | solution.py:488
  41.6 91.7 %collective-permute-start.9 = (bf16[2048,512]{1,0:T(8,128)(2,1)}, bf16[2048,512]{1,0:T(8,128)(2,1)}, u32[]{:S(2)}, u32[]{:S(2)}) collective-permute-start(bf16[2048,512]{1,0:T(8,128)(2,1)} %get-tuple-element.119), channel_id=1, source_target_pairs={{0,2},{1,3},{2,0},{3,1},{4,6},{5,7},{6,4},{7,5}} | collective-permute-start | bytes 6291464 | tf_op jit(solution)/shard_map/ppermute | solution.py:488
  124.5 194.7 %collective-permute-start.7 = (bf16[8192,512]{1,0:T(8,128)(2,1)}, bf16[8192,512]{1,0:T(8,128)(2,1)}, u32[]{:S(2)}, u32[]{:S(2)}) collective-permute-start(bf16[8192,512]{1,0:T(8,128)(2,1)} %x_ref.3), channel_id=1, source_target_pairs={{0,2},{1,3},{2,0},{3,1},{4,6},{5,7},{6,4},{7,5}} | collective-permute-start | bytes 25165832 | tf_op jit(solution)/shard_map/ppermute | solution.py:488
  130.7 183.7 %collective-permute-start.6 = (f32[3,8,640]{2,1,0:T(8,128)}, f32[3,8,640]{2,1,0:T(8,128)}, u32[]{:S(2)}, u32[]{:S(2)}) collective-permute-start(f32[3,8,640]{2,1,0:T(8,128)} %get-tuple-element.153), channel_id=1, source_target_pairs={{0,2},{1,3},{2,0},{3,1},{4,6},{5,7},{6,4},{7,5}} | collective-permute-start | bytes 184328 | tf_op jit(solution)/shard_map/ppermute | solution.py:488
  133.3 218.5 %collective-permute-start.14 = (f32[3,8,640]{2,1,0:T(8,128)}, f32[3,8,640]{2,1,0:T(8,128)}, u32[]{:S(2)}, u32[]{:S(2)}) collective-permute-start(f32[3,8,640]{2,1,0:T(8,128)} %get-tuple-element.152), channel_id=1, source_target_pairs={{0,3},{1,2},{2,1},{3,0},{4,7},{5,6},{6,5},{7,4}} | collective-permute-start | bytes 184328 | tf_op jit(solution)/shard_map/ppermute | solution.py:488
  134.1 184.5 %collective-permute-start.10 = (bf16[2048,512]{1,0:T(8,128)(2,1)}, bf16[2048,512]{1,0:T(8,128)(2,1)}, u32[]{:S(2)}, u32[]{:S(2)}) collective-permute-start(bf16[2048,512]{1,0:T(8,128)(2,1)} %collective-permute-done.8.refs_0_), channel_id=1, source_target_pairs={{0,4},{4,0},{1,5},{5,1},{2,6},{6,2},{3,7},{7,3}} | collective-permute-start | bytes 6291464 | tf_op jit(solution)/shard_map/ppermute | solution.py:491
  135.7 183.5 %collective-permute-start.11 = (bf16[2048,512]{1,0:T(8,128)(2,1)}, bf16[2048,512]{1,0:T(8,128)(2,1)}, u32[]{:S(2)}, u32[]{:S(2)}) collective-permute-start(bf16[2048,512]{1,0:T(8,128)(2,1)} %collective-permute-done.9.refs_1_), channel_id=1, source_target_pairs={{0,4},{4,0},{1,5},{5,1},{2,6},{6,2},{3,7},{7,3}} | collective-permute-start | bytes 6291464 | tf_op jit(solution)/shard_map/ppermute | solution.py:491
  314.4 90.5 %collective-permute-start.16 = (bf16[2048,512]{1,0:T(8,128)(2,1)}, bf16[2048,512]{1,0:T(8,128)(2,1)}, u32[]{:S(2)}, u32[]{:S(2)}) collective-permute-start(bf16[2048,512]{1,0:T(8,128)(2,1)} %collective-permute-done.8.refs_0_), channel_id=1, source_target_pairs={{0,1},{1,0},{2,3},{3,2},{4,5},{5,4},{6,7},{7,6}} | collective-permute-start | bytes 6291464 | tf_op jit(solution)/shard_map/ppermute | solution.py:488
  318.7 88.3 %collective-permute-start.17 = (bf16[2048,512]{1,0:T(8,128)(2,1)}, bf16[2048,512]{1,0:T(8,128)(2,1)}, u32[]{:S(2)}, u32[]{:S(2)}) collective-permute-start(bf16[2048,512]{1,0:T(8,128)(2,1)} %collective-permute-done.9.refs_1_), channel_id=1, source_target_pairs={{0,1},{1,0},{2,3},{3,2},{4,5},{5,4},{6,7},{7,6}} | collective-permute-start | bytes 6291464 | tf_op jit(solution)/shard_map/ppermute | solution.py:488
  319.2 87.8 %collective-permute-start.18 = (bf16[2048,512]{1,0:T(8,128)(2,1)}, bf16[2048,512]{1,0:T(8,128)(2,1)}, u32[]{:S(2)}, u32[]{:S(2)}) collective-permute-start(bf16[2048,512]{1,0:T(8,128)(2,1)} %collective-permute-done.10.refs_2_), channel_id=1, source_target_pairs={{0,1},{1,0},{2,3},{3,2},{4,5},{5,4},{6,7},{7,6}} | collective-permute-start | bytes 6291464 | tf_op jit(solution)/shard_map/ppermute | solution.py:488
  319.2 89.8 %collective-permute-start.15 = (bf16[8192,512]{1,0:T(8,128)(2,1)}, bf16[8192,512]{1,0:T(8,128)(2,1)}, u32[]{:S(2)}, u32[]{:S(2)}) collective-permute-start(bf16[8192,512]{1,0:T(8,128)(2,1)} %collective-permute-done.7.x_ref), channel_id=1, source_target_pairs={{0,1},{1,0},{2,3},{3,2},{4,5},{5,4},{6,7},{7,6}} | collective-permute-start | bytes 25165832 | tf_op jit(solution)/shard_map/ppermute | solution.py:488
  351.8 57.2 %collective-permute-start.19 = (bf16[2048,512]{1,0:T(8,128)(2,1)}, bf16[2048,512]{1,0:T(8,128)(2,1)}, u32[]{:S(2)}, u32[]{:S(2)}) collective-permute-start(bf16[2048,512]{1,0:T(8,128)(2,1)} %collective-permute-done.11.refs_3_), channel_id=1, source_target_pairs={{0,1},{1,0},{2,3},{3,2},{4,5},{5,4},{6,7},{7,6}} | collective-permute-start | bytes 6291464 | tf_op jit(solution)/shard_map/ppermute | solution.py:488
  404.9 290.4 %collective-permute-start = (bf16[8,640,256]{2,1,0:T(8,128)(2,1)}, bf16[8,640,256]{2,1,0:T(8,128)(2,1)}, u32[]{:S(2)}, u32[]{:S(2)}) collective-permute-start(bf16[8,640,256]{2,1,0:T(8,128)(2,1)} %get-tuple-element.61), channel_id=1, source_target_pairs={{0,4},{4,0},{1,5},{5,1},{2,6},{6,2},{3,7},{7,3}} | collective-permute-start | bytes 7864328 | tf_op jit(solution)/shard_map/ppermute | solution.py:491
  406.9 290.3 %collective-permute-start.23 = (bf16[8,640,256]{2,1,0:T(8,128)(2,1)}, bf16[8,640,256]{2,1,0:T(8,128)(2,1)}, u32[]{:S(2)}, u32[]{:S(2)}) collective-permute-start(bf16[8,640,256]{2,1,0:T(8,128)(2,1)} %get-tuple-element.85), channel_id=1, source_target_pairs={{0,4},{4,0},{1,5},{5,1},{2,6},{6,2},{3,7},{7,3}} | collective-permute-start | bytes 7864328 | tf_op jit(solution)/shard_map/ppermute | solution.py:491
  407.0 170.4 %collective-permute-start.4 = (bf16[8,640,256]{2,1,0:T(8,128)(2,1)}, bf16[8,640,256]{2,1,0:T(8,128)(2,1)}, u32[]{:S(2)}, u32[]{:S(2)}) collective-permute-start(bf16[8,640,256]{2,1,0:T(8,128)(2,1)} %get-tuple-element.65), channel_id=1, source_target_pairs={{0,4},{4,0},{1,5},{5,1},{2,6},{6,2},{3,7},{7,3}} | collective-permute-start | bytes 7864328 | tf_op jit(solution)/shard_map/ppermute | solution.py:491
  409.0 224.5 %collective-permute-start.12 = (bf16[8,640,256]{2,1,0:T(8,128)(2,1)}, bf16[8,640,256]{2,1,0:T(8,128)(2,1)}, u32[]{:S(2)}, u32[]{:S(2)}) collective-permute-start(bf16[8,640,256]{2,1,0:T(8,128)(2,1)} %get-tuple-element.77), channel_id=1, source_target_pairs={{0,4},{4,0},{1,5},{5,1},{2,6},{6,2},{3,7},{7,3}} | collective-permute-start | bytes 7864328 | tf_op jit(solution)/shard_map/ppermute | solution.py:491
  490.2 199.4 %collective-permute-start.20 = (bf16[8,640,256]{2,1,0:T(8,128)(2,1)}, bf16[8,640,256]{2,1,0:T(8,128)(2,1)S(1)}, u32[]{:S(2)}, u32[]{:S(2)}) collective-permute-start(bf16[8,640,256]{2,1,0:T(8,128)(2,1)} %get-tuple-element.82), channel_id=1, source_target_pairs={{0,4},{4,0},{1,5},{5,1},{2,6},{6,2},{3,7},{7,3}} | collective-permute-start | bytes 7864328 | tf_op jit(solution)/shard_map/ppermute | solution.py:491
  577.3 168.5 %collective-permute-start.24 = (bf16[8,640,256]{2,1,0:T(8,128)(2,1)}, bf16[8,640,256]{2,1,0:T(8,128)(2,1)}, u32[]{:S(2)}, u32[]{:S(2)}) collective-permute-start(bf16[8,640,256]{2,1,0:T(8,128)(2,1)} %get-tuple-element.87), channel_id=1, source_target_pairs={{0,4},{4,0},{1,5},{5,1},{2,6},{6,2},{3,7},{7,3}} | collective-permute-start | bytes 7864328 | tf_op jit(solution)/shard_map/ppermute | solution.py:491
  633.5 168.3 %collective-permute-start.26 = (bf16[8,640,256]{2,1,0:T(8,128)(2,1)}, bf16[8,640,256]{2,1,0:T(8,128)(2,1)}, u32[]{:S(2)}, u32[]{:S(2)}) collective-permute-start(bf16[8,640,256]{2,1,0:T(8,128)(2,1)} %get-tuple-element.89), channel_id=1, source_target_pairs={{0,4},{4,0},{1,5},{5,1},{2,6},{6,2},{3,7},{7,3}} | collective-permute-start | bytes 7864328 | tf_op jit(solution)/shard_map/ppermute | solution.py:491
  689.6 117.9 %collective-permute-start.5 = (bf16[8,640,256]{2,1,0:T(8,128)(2,1)}, bf16[8,640,256]{2,1,0:T(8,128)(2,1)}, u32[]{:S(2)}, u32[]{:S(2)}) collective-permute-start(bf16[8,640,256]{2,1,0:T(8,128)(2,1)} %add_convert_fusion.6), channel_id=1, source_target_pairs={{0,1},{1,0},{2,3},{3,2},{4,5},{5,4},{6,7},{7,6}} | collective-permute-start | bytes 7864328 | tf_op jit(solution)/shard_map/ppermute | solution.py:488
  695.3 113.8 %collective-permute-start.13 = (bf16[8,640,256]{2,1,0:T(8,128)(2,1)}, bf16[8,640,256]{2,1,0:T(8,128)(2,1)}, u32[]{:S(2)}, u32[]{:S(2)}) collective-permute-start(bf16[8,640,256]{2,1,0:T(8,128)(2,1)} %add_convert_fusion.5), channel_id=1, source_target_pairs={{0,2},{1,3},{2,0},{3,1},{4,6},{5,7},{6,4},{7,5}} | collective-permute-start | bytes 7864328 | tf_op jit(solution)/shard_map/ppermute | solution.py:488
  697.3 113.5 %collective-permute-start.21 = (bf16[8,640,256]{2,1,0:T(8,128)(2,1)}, bf16[8,640,256]{2,1,0:T(8,128)(2,1)}, u32[]{:S(2)}, u32[]{:S(2)}) collective-permute-start(bf16[8,640,256]{2,1,0:T(8,128)(2,1)} %add_convert_fusion.4), channel_id=1, source_target_pairs={{0,3},{1,2},{2,1},{3,0},{4,7},{5,6},{6,5},{7,4}} | collective-permute-start | bytes 7864328 | tf_op jit(solution)/shard_map/ppermute | solution.py:488
  750.7 122.4 %collective-permute-start.25 = (bf16[8,640,256]{2,1,0:T(8,128)(2,1)}, bf16[8,640,256]{2,1,0:T(8,128)(2,1)}, u32[]{:S(2)}, u32[]{:S(2)}) collective-permute-start(bf16[8,640,256]{2,1,0:T(8,128)(2,1)} %add_convert_fusion.2), channel_id=1, source_target_pairs={{0,1},{1,0},{2,3},{3,2},{4,5},{5,4},{6,7},{7,6}} | collective-permute-start | bytes 7864328 | tf_op jit(solution)/shard_map/ppermute | solution.py:488
  805.8 67.3 %collective-permute-start.27 = (bf16[8,640,256]{2,1,0:T(8,128)(2,1)}, bf16[8,640,256]{2,1,0:T(8,128)(2,1)}, u32[]{:S(2)}, u32[]{:S(2)}) collective-permute-start(bf16[8,640,256]{2,1,0:T(8,128)(2,1)} %add_convert_fusion.1), channel_id=1, source_target_pairs={{0,2},{1,3},{2,0},{3,1},{4,6},{5,7},{6,4},{7,5}} | collective-permute-start | bytes 7864328 | tf_op jit(solution)/shard_map/ppermute | solution.py:488
  807.5 59.4 %collective-permute-start.28 = (bf16[8,640,256]{2,1,0:T(8,128)(2,1)}, bf16[8,640,256]{2,1,0:T(8,128)(2,1)}, u32[]{:S(2)}, u32[]{:S(2)}) collective-permute-start(bf16[8,640,256]{2,1,0:T(8,128)(2,1)} %get-tuple-element.91), channel_id=1, source_target_pairs={{0,4},{4,0},{1,5},{5,1},{2,6},{6,2},{3,7},{7,3}} | collective-permute-start | bytes 7864328 | tf_op jit(solution)/shard_map/ppermute | solution.py:491
  870.2 57.4 %collective-permute-start.29 = (bf16[8,640,256]{2,1,0:T(8,128)(2,1)S(1)}, bf16[8,640,256]{2,1,0:T(8,128)(2,1)S(1)}, u32[]{:S(2)}, u32[]{:S(2)}) collective-permute-start(bf16[8,640,256]{2,1,0:T(8,128)(2,1)S(1)} %add_convert_fusion), channel_id=1, source_target_pairs={{0,3},{1,2},{2,1},{3,0},{4,7},{5,6},{6,5},{7,4}} | collective-permute-start | bytes 7864328 | tf_op jit(solution)/shard_map/ppermute | solution.py:488
  986.7 96.7 %collective-permute-start.22 = (bf16[8192,256]{1,0:T(8,128)(2,1)}, bf16[8192,256]{1,0:T(8,128)(2,1)}, u32[]{:S(2)}, u32[]{:S(2)}) collective-permute-start(bf16[8192,256]{1,0:T(8,128)(2,1)} %get-tuple-element.83), channel_id=1, source_target_pairs={{0,4},{4,0},{1,5},{5,1},{2,6},{6,2},{3,7},{7,3}} | collective-permute-start | bytes 12582920 | tf_op jit(solution)/shard_map/ppermute | solution.py:491
  989.8 91.6 %collective-permute-start.35 = (f32[33,256]{1,0:T(8,128)}, f32[33,256]{1,0:T(8,128)}, u32[]{:S(2)}, u32[]{:S(2)}) collective-permute-start(f32[33,256]{1,0:T(8,128)} %add.302), channel_id=1, source_target_pairs={{0,4},{4,0},{1,5},{5,1},{2,6},{6,2},{3,7},{7,3}} | collective-permute-start | bytes 101384 | tf_op jit(solution)/shard_map/ppermute | solution.py:491
  1006.5 163.7 %collective-permute-start.32 = (bf16[8192,256]{1,0:T(8,128)(2,1)}, bf16[8192,256]{1,0:T(8,128)(2,1)}, u32[]{:S(2)}, u32[]{:S(2)}) collective-permute-start(bf16[8192,256]{1,0:T(8,128)(2,1)} %finish_dx.1), channel_id=1, source_target_pairs={{0,4},{4,0},{1,5},{5,1},{2,6},{6,2},{3,7},{7,3}} | collective-permute-start | bytes 12582920 | tf_op jit(solution)/shard_map/ppermute | solution.py:491
  (52 other events, 601.0 us)
